TPU v7x, 16 devices: a 4x2x1 block of a 4x4x8 slice. The times are simulated.
16 devices in a mesh: dp: 2 (over y, z), ep: 8 (over x, core).
Axes of the slice: x: 4, y: 2, z: 1, core: 2. Of those that a mesh axis runs over, the one named last changes fastest.
The devices are a block of a 4x4x8 slice.
Arguments:
- x_in: bfloat16 [2048, 2048], P(('dp', 'ep')), parts along dimension 0
- k_cache: bfloat16 [2048, 32, 4, 128], P(('dp', 'ep')), parts along dimension 0
- v_cache: bfloat16 [2048, 32, 4, 128], P(('dp', 'ep')), parts along dimension 0
- cache_len: int32 [2048], P(('dp', 'ep')), parts along dimension 0
- topk_idx: int32 [2048, 8], P(('dp', 'ep')), parts along dimension 0
- ln_attn: bfloat16 [2048], replicated
- w_q: bfloat16 [2048, 4096], replicated
- w_k: bfloat16 [2048, 512], replicated
- w_v: bfloat16 [2048, 512], replicated
- q_norm: bfloat16 [128], replicated
- k_norm: bfloat16 [128], replicated
- w_o: bfloat16 [4096, 2048], replicated
- ln_moe: bfloat16 [2048], replicated
- w_router: bfloat16 [2048, 128], replicated
- w_gate: bfloat16 [128, 2048, 768], P('ep')
- w_up: bfloat16 [128, 2048, 768], P('ep')
- w_down: bfloat16 [128, 768, 2048], P('ep')
Outputs:
- output 1: bfloat16 [2048, 2048], P(('dp', 'ep')), parts along dimension 0
- output 2: bfloat16 [2048, 32, 4, 128], P(('dp', 'ep')), parts along dimension 0
- output 3: bfloat16 [2048, 32, 4, 128], P(('dp', 'ep')), parts along dimension 0
There are 2 independent parts. A program takes and returns all parts, laid end to end along the dimension named above; an argument that names none is the same for every part.
All inputs are finite; a program needn't handle non-finite values.
Results may differ from a plain program's by a relative error of at most 0.0142757.
Values are sent between devices in bfloat16 or wider.
A program may use at most 768 MiB of HBM per device.

v0:
```python
import jax
import jax.numpy as jnp
from jax import lax
from jax.sharding import PartitionSpec as P

ROPE_BASE = 1000000.0
NORM_EPS = 1e-6


def norm_scale(values, gain_vec):
    return values * lax.rsqrt(jnp.mean(values * values, axis=-1, keepdims=True) + NORM_EPS) * gain_vec.astype(jnp.float32)


def rotate_halves(values, positions):
    half_dim = values.shape[-1] // 2
    freq_vec = ROPE_BASE ** (-jnp.arange(half_dim, dtype=jnp.float32) * 2.0 / values.shape[-1])
    angles = positions.astype(jnp.float32)[:, None, None] * freq_vec
    cosine = jnp.cos(angles)
    sine_val = jnp.sin(angles)
    lo_half = values[..., :half_dim]
    hi_half = values[..., half_dim:]
    return jnp.concatenate([lo_half * cosine - hi_half * sine_val, hi_half * cosine + lo_half * sine_val], axis=-1)


def attend_block(x_in, k_cache, v_cache, cache_len, ln_attn, w_q, w_k, w_v, q_norm, k_norm, w_o):
    n_batch, n_slots, kv_heads, head_dim = k_cache.shape
    q_heads = w_q.shape[1] // head_dim
    resid_in = x_in.astype(jnp.float32)
    normed = norm_scale(resid_in, ln_attn).astype(jnp.bfloat16)
    q_proj = jnp.dot(normed, w_q, preferred_element_type=jnp.float32).reshape(n_batch, q_heads, head_dim)
    k_proj = jnp.dot(normed, w_k, preferred_element_type=jnp.float32).reshape(n_batch, kv_heads, head_dim)
    v_new = jnp.dot(normed, w_v, preferred_element_type=jnp.float32).astype(jnp.bfloat16).reshape(n_batch, kv_heads, head_dim)
    q_rot = rotate_halves(norm_scale(q_proj, q_norm), cache_len).astype(jnp.bfloat16).reshape(n_batch, kv_heads, q_heads // kv_heads, head_dim)
    k_new = rotate_halves(norm_scale(k_proj, k_norm), cache_len).astype(jnp.bfloat16)
    len_col = cache_len[:, None, None, None]
    is_new = lax.broadcasted_iota(jnp.int32, (1, n_slots, 1, 1), 1) == len_col
    k_full = jnp.where(is_new, k_new[:, None], k_cache)
    v_full = jnp.where(is_new, v_new[:, None], v_cache)
    scores = jnp.einsum('bgrd,bsgd->bgrs', q_rot, k_full, preferred_element_type=jnp.float32) * head_dim ** -0.5
    seen = lax.broadcasted_iota(jnp.int32, (1, 1, 1, n_slots), 3) <= len_col
    attn_prob = jax.nn.softmax(jnp.where(seen, scores, -1e30), axis=-1).astype(jnp.bfloat16)
    attn_out = jnp.einsum('bgrs,bsgd->bgrd', attn_prob, v_full, preferred_element_type=jnp.float32).astype(jnp.bfloat16).reshape(n_batch, q_heads * head_dim)
    x_mid = (resid_in + jnp.dot(attn_out, w_o, preferred_element_type=jnp.float32)).astype(jnp.bfloat16)
    return x_mid, k_full, v_full


def route_gate(x_mid, ln_moe, w_router, topk_idx):
    resid_mid = x_mid.astype(jnp.float32)
    h_moe = norm_scale(resid_mid, ln_moe).astype(jnp.bfloat16)
    logits = jnp.dot(h_moe, w_router, preferred_element_type=jnp.float32)
    gate_wts = jax.nn.softmax(jnp.take_along_axis(logits, topk_idx, axis=1), axis=-1)
    return resid_mid, h_moe, gate_wts


def pack_rows(h_moe, topk_idx, ep_size, e_local, cap_rows):
    b_dev, top_k = topk_idx.shape
    pair_count = b_dev * top_k
    flat_idx = topk_idx.reshape(pair_count)
    dest_dev = flat_idx // e_local
    dest_hot = (dest_dev[:, None] == jnp.arange(ep_size)[None, :]).astype(jnp.int32)
    dev_counts = jnp.sum(dest_hot, axis=0)
    slot_rank = jnp.sum(jnp.cumsum(dest_hot, axis=0) * dest_hot, axis=1) - 1
    dev_start = jnp.cumsum(dev_counts) - dev_counts
    sort_order = jnp.argsort(dest_dev, stable=True)
    seat_ids = jnp.arange(cap_rows)
    pair_at = sort_order[jnp.minimum(dev_start[:, None] + seat_ids[None, :], pair_count - 1)]
    filled = seat_ids[None, :] < dev_counts[:, None]
    send_rows = jnp.where(filled[:, :, None], h_moe[pair_at // top_k], jnp.zeros((), jnp.bfloat16))
    send_ids = jnp.where(filled, (flat_idx % e_local)[pair_at], e_local - 1)
    return send_rows, send_ids, dest_dev * cap_rows + slot_rank


def group_count(row_ids, e_local):
    return jnp.sum((row_ids[:, None] == jnp.arange(e_local)[None, :]).astype(jnp.int32), axis=0)


def expert_sorted(sorted_rows, group_sizes, w_gate, w_up, w_down):
    gate_act = lax.ragged_dot(sorted_rows, w_gate, group_sizes, preferred_element_type=jnp.float32)
    up_act = lax.ragged_dot(sorted_rows, w_up, group_sizes, preferred_element_type=jnp.float32)
    hidden_act = (jax.nn.silu(gate_act) * up_act).astype(jnp.bfloat16)
    return lax.ragged_dot(hidden_act, w_down, group_sizes, preferred_element_type=jnp.float32).astype(jnp.bfloat16)


def expert_rows(tok_rows, row_ids, w_gate, w_up, w_down):
    sort_order = jnp.argsort(row_ids, stable=True)
    sorted_out = expert_sorted(tok_rows[sort_order], group_count(row_ids, w_gate.shape[0]), w_gate, w_up, w_down)
    return sorted_out[jnp.argsort(sort_order, stable=True)]


def unpack_rows(back_rows, flat_slot, gate_wts):
    b_dev, top_k = gate_wts.shape
    picked = back_rows[flat_slot].reshape(b_dev, top_k, back_rows.shape[1])
    return jnp.sum(picked.astype(jnp.float32) * gate_wts[:, :, None], axis=1)


def solution(mesh):
    ep_size = mesh.shape['ep']
    row_spec = P(('dp', 'ep'))
    replicated = P()
    expert_spec = P('ep')
    in_specs = (row_spec, row_spec, row_spec, row_spec, row_spec, replicated, replicated, replicated, replicated, replicated, replicated, replicated, replicated, replicated, expert_spec, expert_spec, expert_spec)
    out_specs = (row_spec, row_spec, row_spec)

    def device_step(x_in, k_cache, v_cache, cache_len, topk_idx, ln_attn, w_q, w_k, w_v, q_norm, k_norm, w_o, ln_moe, w_router, w_gate, w_up, w_down):
        x_mid, k_full, v_full = attend_block(x_in, k_cache, v_cache, cache_len, ln_attn, w_q, w_k, w_v, q_norm, k_norm, w_o)
        resid_mid, h_moe, gate_wts = route_gate(x_mid, ln_moe, w_router, topk_idx)
        b_dev, top_k = topk_idx.shape
        hidden = h_moe.shape[1]
        e_local = w_gate.shape[0]
        cap_rows = min(b_dev, 2 * b_dev * top_k // ep_size)
        send_rows, send_ids, flat_slot = pack_rows(h_moe, topk_idx, ep_size, e_local, cap_rows)
        recv_rows = lax.all_to_all(send_rows, 'ep', 0, 0, tiled=True).reshape(ep_size * cap_rows, hidden)
        recv_ids = lax.all_to_all(send_ids, 'ep', 0, 0, tiled=True).reshape(ep_size * cap_rows)
        expert_out = expert_rows(recv_rows, recv_ids, w_gate, w_up, w_down)
        back_rows = lax.all_to_all(expert_out.reshape(ep_size, cap_rows, hidden), 'ep', 0, 0, tiled=True).reshape(ep_size * cap_rows, hidden)
        moe_out = unpack_rows(back_rows, flat_slot, gate_wts)
        return (resid_mid + moe_out).astype(jnp.bfloat16), k_full, v_full

    return jax.shard_map(device_step, mesh=mesh, in_specs=in_specs, out_specs=out_specs, check_vma=False)
```

profile of v0, /device:TPU:113, one launch (start us, length us, event | category | flops | bytes accessed | tf_op | source)
XLA Modules:
  0.0 339.6 jit_solution(5331923728664360915)
XLA Ops:
  0.6 0.9 copy.56
  1.8 2.3 reduce-window.19
  4.1 0.3 slice_reduce_fusion
  4.6 4.4 %sort.45 = (s32[1024]{0:T(1024)}, s32[1024]{0:T(1024)S(1)}) sort(s32[1024]{0:T(1024)S(1)} %get-tuple-element.31, s32[1024]{0:T(1024)S(1)} %iota.60), dimensions={0}, to_apply=%region_7.8 | sort | flops 10240 | bytes 16384 | tf_op jit(solution)/shard_map/jit(argsort)/sort | solution.py:64
  9.1 0.2 reduce-window.18
  9.4 4.5 %gather_fusion = s32[1024]{0:T(1024)S(1)} fusion(s32[1024]{0:T(1024)S(1)} %get-tuple-element.6, s32[1024]{0:T(1024)S(1)} %fusion.34), kind=kCustom, calls=%fused_computation | custom fusion | bytes 12288 | tf_op jit(solution)/shard_map/gather | solution.py:66
  14.0 4.5 %gather_fusion.2 = s32[1024]{0:T(1024)S(1)} fusion(s32[1024]{0:T(1024)S(1)} %get-tuple-element.32, s32[1024]{0:T(1024)S(1)} %get-tuple-element.30), kind=kCustom, calls=%fused_computation.2 | custom fusion | bytes 12288 | tf_op jit(solution)/shard_map/gather | solution.py:69
  18.5 0.7 compare_select_fusion.1
  19.2 6.0 %all-to-all-start.1 = ((s32[8,1,128]{2,1,0:T(1,128)}), s32[8,1,128]{2,1,0:T(1,128)S(1)}, u32[]{:S(2)}, u32[]{:S(2)}) async-start(s32[8,1,128]{2,1,0:T(1,128)} %compare_select_fusion.1), calls=%async_computation.1 | async-start | bytes 8192 | tf_op jit(solution)/shard_map/all_to_all | solution.py:113
  25.5 0.2 fusion.12
  25.7 0.5 convolution_convert_fusion
  26.3 2.1 fusion.51
  28.5 0.2 multiply_reduce_fusion.2
  28.7 8.2 %convolution_bitcast_fusion = f32[16,8,32,128]{3,1,2,0:T(8,128)S(1)} fusion(bf16[2048,4096]{1,0:T(8,128)(2,1)} %param.23, bf16[128,2048]{1,0:T(8,128)(2,1)S(1)} %copy-done.2, f32[2048]{0:T(1024)S(1)} %convert_element_type.73, f32[128]{0:T(128)S(1)} %add_rsqrt_fusion.3), kind=kOutput, calls=%fused_computation.29 | convolution fusion | flops 2148532224 | bytes 19407360 | tf_op jit(solution)/shard_map/dot_general | solution.py:30
  36.9 0.4 copy.62
  37.3 0.6 multiply_reduce_fusion
  38.0 0.3 multiply_cosine_fusion
  38.3 0.2 multiply_multiply_fusion.1
  38.5 0.9 multiply_multiply_fusion
  39.4 0.3 subtract_convert_fusion.1
  39.7 0.8 fusion.15
  40.7 1.5 copy-done.5
  42.2 6.8 %broadcast_select_fusion.2 = (bf16[128,32,4,128]{3,2,1,0:T(4,128)(2,1)}, bf16[128,32,4,128]{3,2,1,0:T(4,128)(2,1)}) fusion(bf16[128,32,4,128]{3,2,1,0:T(4,128)(2,1)S(1)} %copy-done.5, pred[128,32]{1,0:T(8,128)(4,1)S(1)} %get-tuple-element.36, bf16[128,4,128]{2,1,0:T(4,128)(2,1)S(1)} %pad_maximum_fusion, bf16[128,32,4,128]{3,2,1,0:T(4,128)(2,1)S(1)} %copy-done.6, ...), kind=kLoop, calls=%fused_computation.16 | loop fusion | flops 4194304 | bytes 17043456 | tf_op jit(solution)/shard_map/jit(_where)/select_n | solution.py:37
  48.9 6.2 %fusion.54 = (f32[128,4,8]{2,1,0:T(4,128)S(1)}, f32[128,4,8,32]{3,2,1,0:T(8,128)}) fusion(pred[128,32]{1,0:T(8,128)(4,1)S(1)} %get-tuple-element.35, bf16[128,32,4,128]{3,2,1,0:T(4,128)(2,1)} %get-tuple-element.27, bf16[128,4,8,64]{3,2,1,0:T(8,128)(2,1)S(1)} %get-tuple-element.24, bf16[128,4,8,64]{3,2,1,0:T(8,128)(2,1)S(1)} %get-tuple-element.23), kind=kOutput, calls=%fused_computation.134 | convolution fusion | flops 36175904 | bytes 5787648 | tf_op jit(solution)/shard_map/sub | solution.py:41
  55.1 4.1 %fusion.9 = bf16[128,4,8,128]{3,2,1,0:T(8,128)(2,1)S(1)} fusion(bf16[128,32,4,128]{3,2,1,0:T(4,128)(2,1)} %get-tuple-element.28, f32[128,4,8,32]{3,2,1,0:T(8,128)} %get-tuple-element.38, f32[128,4,8]{2,1,0:T(4,128)S(1)} %get-tuple-element.37), kind=kOutput, calls=%fused_computation.32 | convolution fusion | flops 34340864 | bytes 5783552 | tf_op jit(solution)/shard_map/bgrs,bsgd->bgrd/dot_general | solution.py:42
  59.2 8.5 %multiply_reduce_fusion.1 = (f32[128]{0:T(128)S(1)}, f32[128,2048]{1,0:T(8,128)S(1)}) fusion(bf16[4096,2048]{1,0:T(8,128)(2,1)} %param.28, bf16[16,8,32,128]{3,2,1,0:T(8,128)(2,1)S(1)} %bitcast.88, bf16[128,2048]{1,0:T(8,128)(2,1)S(1)} %copy-done.2), kind=kOutput, calls=%fused_computation.46 | convolution fusion | flops 2149056512 | bytes 19399168 | tf_op jit(solution)/shard_map/dot_general | solution.py:43
  67.9 6.0 %gather_fusion.1 = bf16[1024,2048]{1,0:T(8,128)(2,1)} fusion(bf16[128,2048]{1,0:T(8,128)(2,1)S(1)} %multiply_convert_fusion.1, s32[1024]{0:T(1024)S(1)} %get-tuple-element.29), kind=kCustom, calls=%fused_computation.1 | custom fusion | bytes 8392704 | tf_op jit(solution)/shard_map/gather | solution.py:68
  73.9 4.5 %broadcast_select_fusion = bf16[8,128,2048]{2,1,0:T(8,128)(2,1)} fusion(bf16[8,128,2048]{2,1,0:T(8,128)(2,1)} %bitcast.87, pred[8,128]{1,0:T(8,128)(4,1)S(1)} %iota_compare_fusion.5), kind=kLoop, calls=%fused_computation.14 | loop fusion | flops 2097152 | bytes 8389632 | tf_op jit(solution)/shard_map/jit(_where)/select_n | solution.py:68
  78.4 4.8 %all-to-all-start = ((bf16[8,128,2048]{2,1,0:T(8,128)(2,1)}), bf16[8,128,2048]{2,1,0:T(8,128)(2,1)}, u32[]{:S(2)}, u32[]{:S(2)}) async-start(bf16[8,128,2048]{2,1,0:T(8,128)(2,1)} %broadcast_select_fusion), calls=%async_computation | async-start | bytes 8388608 | tf_op jit(solution)/shard_map/all_to_all | solution.py:112
  83.3 4.4 %sort.46 = (s32[1024]{0:T(1024)}, s32[1024]{0:T(1024)S(1)}) sort(s32[1024]{0:T(1024)S(1)} %bitcast.89, s32[1024]{0:T(1024)S(1)} %iota.61), dimensions={0}, to_apply=%region_9.10 | sort | flops 10240 | bytes 16384 | tf_op jit(solution)/shard_map/jit(argsort)/sort | solution.py:85
  87.6 0.6 convert_reduce_fusion
  88.3 1.8 ragged-dot-metadata
  90.1 4.4 %sort.47 = (s32[1024]{0:T(1024)}, s32[1024]{0:T(1024)S(1)}) sort(s32[1024]{0:T(1024)S(1)} %get-tuple-element.7, s32[1024]{0:T(1024)S(1)} %iota.62), dimensions={0}, to_apply=%region_11.12 | sort | flops 10240 | bytes 16384 | tf_op jit(solution)/shard_map/jit(argsort)/sort | solution.py:87
  94.4 37.4 %all-to-all-done = bf16[8,128,2048]{2,1,0:T(8,128)(2,1)} async-done(((bf16[8,128,2048]{2,1,0:T(8,128)(2,1)}), bf16[8,128,2048]{2,1,0:T(8,128)(2,1)}, u32[]{:S(2)}, u32[]{:S(2)}) %all-to-all-start) | async-done | bytes 4194336 | tf_op jit(solution)/shard_map/all_to_all | solution.py:112
  131.8 11.6 %gather_fusion.3 = bf16[1024,2048]{1,0:T(8,128)(2,1)} fusion(bf16[1024,2048]{1,0:T(8,128)(2,1)} %bitcast.11, s32[1024]{0:T(1024)S(1)} %fusion.37), kind=kCustom, calls=%fused_computation.3 | custom fusion | bytes 8392704 | tf_op jit(solution)/shard_map/gather | solution.py:86
  143.4 32.8 %ragged-dot-none.2 = f32[1024,768]{1,0:T(8,128)} custom-call(s32[1]{0:T(128)} %get-tuple-element.9, s32[17]{0:T(128)} %get-tuple-element.10, s32[19]{0:T(128)} %get-tuple-element.11, s32[19]{0:T(128)} %get-tuple-element.12, s32[1]{0:T(128)} %get-tuple-element.9, bf16[1024,2048]{1,0:T(8,128)(2,1)} %gather_fusion.3, bf16[16,2048,768]{2,1,0:T(8,128)(2,1)} %param.31), custom_call_target="tpu_custom_call" | custom-call | flops 3221225472 | bytes 57671744 | tf_op jit(solution)/shard_map/ragged_dot_general/ragged-dot-none
  176.2 32.9 %ragged-dot-none.1 = f32[1024,768]{1,0:T(8,128)} custom-call(s32[1]{0:T(128)} %get-tuple-element.9, s32[17]{0:T(128)} %get-tuple-element.10, s32[19]{0:T(128)} %get-tuple-element.11, s32[19]{0:T(128)} %get-tuple-element.12, s32[1]{0:T(128)} %get-tuple-element.9, bf16[1024,2048]{1,0:T(8,128)(2,1)} %gather_fusion.3, bf16[16,2048,768]{2,1,0:T(8,128)(2,1)} %param.32), custom_call_target="tpu_custom_call" | custom-call | flops 3221225472 | bytes 57671744 | tf_op jit(solution)/shard_map/ragged_dot_general/ragged-dot-none
  209.1 4.9 %multiply_convert_fusion = bf16[1024,768]{1,0:T(8,128)(2,1)} fusion(f32[1024,768]{1,0:T(8,128)} %ragged-dot-none.1, f32[1024,768]{1,0:T(8,128)} %ragged-dot-none.2), kind=kLoop, calls=%fused_computation.17 | loop fusion | flops 4718592 | bytes 7864320 | tf_op jit(solution)/shard_map/convert_element_type | solution.py:80
  214.0 34.4 %ragged-dot-none = f32[1024,2048]{1,0:T(8,128)} custom-call(s32[1]{0:T(128)} %get-tuple-element.9, s32[17]{0:T(128)} %get-tuple-element.10, s32[19]{0:T(128)} %get-tuple-element.11, s32[19]{0:T(128)} %get-tuple-element.12, s32[1]{0:T(128)} %get-tuple-element.9, bf16[1024,768]{1,0:T(8,128)(2,1)} %multiply_convert_fusion, bf16[16,768,2048]{2,1,0:T(8,128)(2,1)} %param.33), custom_call_target="tpu_custom_call" | custom-call | flops 3221225472 | bytes 60293184 | tf_op jit(solution)/shard_map/ragged_dot_general/ragged-dot-none
  248.4 6.0 %convert_element_type.88 = bf16[1024,2048]{1,0:T(8,128)(2,1)} convert(f32[1024,2048]{1,0:T(8,128)} %ragged-dot-none) | non-fusion elementwise | flops 2097152 | bytes 12582912 | tf_op jit(solution)/shard_map/convert_element_type | solution.py:81
  254.4 11.6 %gather_fusion.4 = bf16[1024,2048]{1,0:T(8,128)(2,1)} fusion(bf16[1024,2048]{1,0:T(8,128)(2,1)} %convert_element_type.88, s32[1024]{0:T(1024)S(1)} %fusion.38), kind=kCustom, calls=%fused_computation.4 | custom fusion | bytes 8392704 | tf_op jit(solution)/shard_map/gather | solution.py:87
  266.0 5.7 %all-to-all-start.2 = ((bf16[8,128,2048]{2,1,0:T(8,128)(2,1)}), bf16[8,128,2048]{2,1,0:T(8,128)(2,1)}, u32[]{:S(2)}, u32[]{:S(2)}) async-start(bf16[8,128,2048]{2,1,0:T(8,128)(2,1)} %bitcast.86), calls=%async_computation.2 | async-start | bytes 8388608 | tf_op jit(solution)/shard_map/all_to_all | solution.py:115
  272.0 0.3 fusion.63
  272.3 6.8 %gather_fusion.6 = f32[1024]{0:T(1024)S(1)} fusion(f32[128,128]{1,0:T(8,128)S(1)} %fusion.63, s32[1024]{0:T(1024)S(1)} %reshape.610), kind=kCustom, calls=%fused_computation.6 | custom fusion | bytes 16384 | tf_op jit(solution)/shard_map/jit(take_along_axis)/gather | solution.py:51
  279.5 40.9 %all-to-all-done.2 = bf16[8,128,2048]{2,1,0:T(8,128)(2,1)} async-done(((bf16[8,128,2048]{2,1,0:T(8,128)(2,1)}), bf16[8,128,2048]{2,1,0:T(8,128)(2,1)}, u32[]{:S(2)}, u32[]{:S(2)}) %all-to-all-start.2) | async-done | bytes 4194336 | tf_op jit(solution)/shard_map/all_to_all | solution.py:115
  320.3 11.7 %gather_fusion.5 = bf16[1024,2048]{1,0:T(8,128)(2,1)} fusion(bf16[1024,2048]{1,0:T(8,128)(2,1)} %bitcast.13, s32[1024]{0:T(1024)S(1)} %broadcast_clamp_fusion), kind=kCustom, calls=%fused_computation.5 | custom fusion | bytes 8392704 | tf_op jit(solution)/shard_map/gather | solution.py:92
  332.0 6.6 %fusion.1 = f32[128,2048]{1,0:T(8,128)S(1)} fusion(bf16[1024,2048]{1,0:T(8,128)(2,1)} %gather_fusion.5, f32[128,8]{1,0:T(8,128)S(1)} %copy.61), kind=kLoop, calls=%fused_computation.9 | loop fusion | flops 6029312 | bytes 5246976 | tf_op jit(solution)/shard_map/reduce_sum | solution.py:93
  338.6 0.9 add_convert_fusion.1
  (73 shorter events, 2.1 us)
Async XLA Ops:
  0.6 25.1 %copy-start = (bf16[2048,512]{1,0:T(8,128)(2,1)S(1)}, bf16[2048,512]{1,0:T(8,128)(2,1)}, u32[]{:S(2)}) copy-start(bf16[2048,512]{1,0:T(8,128)(2,1)} %param.25) | copy-start | bytes 6291460
  13.9 11.3 %copy-start.11 = (s32[128]{0:T(128)S(1)}, s32[128]{0:T(128)}, u32[]{:S(2)}) copy-start(s32[128]{0:T(128)} %param.20) | copy-start | bytes 1540
  13.9 11.5 %copy-start.12 = (bf16[128]{0:T(256)(128)(2,1)S(1)}, bf16[128]{0:T(256)(128)(2,1)}, u32[]{:S(2)}) copy-start(bf16[128]{0:T(256)(128)(2,1)} %param.26) | copy-start | bytes 772
  13.9 11.5 %copy-start.13 = (bf16[128]{0:T(256)(128)(2,1)S(1)}, bf16[128]{0:T(256)(128)(2,1)}, u32[]{:S(2)}) copy-start(bf16[128]{0:T(256)(128)(2,1)} %param.27) | copy-start | bytes 772
  13.9 11.5 %copy-start.2 = (bf16[128,2048]{1,0:T(8,128)(2,1)S(1)}, bf16[128,2048]{1,0:T(8,128)(2,1)}, u32[]{:S(2)}) copy-start(bf16[128,2048]{1,0:T(8,128)(2,1)} %param.17) | copy-start | bytes 1572868
  14.0 11.7 %copy-start.9 = (bf16[2048]{0:T(1024)(128)(2,1)S(1)}, bf16[2048]{0:T(1024)(128)(2,1)}, u32[]{:S(2)}) copy-start(bf16[2048]{0:T(1024)(128)(2,1)} %param.22) | copy-start | bytes 12292
  14.0 11.7 %copy-start.10 = (bf16[2048]{0:T(1024)(128)(2,1)S(1)}, bf16[2048]{0:T(1024)(128)(2,1)}, u32[]{:S(2)}) copy-start(bf16[2048]{0:T(1024)(128)(2,1)} %param.29) | copy-start | bytes 12292
  19.2 59.2 %all-to-all-start.1 = ((s32[8,1,128]{2,1,0:T(1,128)}), s32[8,1,128]{2,1,0:T(1,128)S(1)}, u32[]{:S(2)}, u32[]{:S(2)}) async-start(s32[8,1,128]{2,1,0:T(1,128)} %compare_select_fusion.1), calls=%async_computation.1 | async-start | bytes 8192 | tf_op jit(solution)/shard_map/all_to_all | solution.py:113
  38.5 2.2 copy-start.6
  39.7 2.5 copy-start.5
  67.7 6.2 %copy-start.3 = (f32[128,2048]{1,0:T(8,128)}, f32[128,2048]{1,0:T(8,128)S(1)}, u32[]{:S(2)}) copy-start(f32[128,2048]{1,0:T(8,128)S(1)} %get-tuple-element.40) | copy-start | bytes 3145732
  78.4 53.4 %all-to-all-start = ((bf16[8,128,2048]{2,1,0:T(8,128)(2,1)}), bf16[8,128,2048]{2,1,0:T(8,128)(2,1)}, u32[]{:S(2)}, u32[]{:S(2)}) async-start(bf16[8,128,2048]{2,1,0:T(8,128)(2,1)} %broadcast_select_fusion), calls=%async_computation | async-start | bytes 8388608 | tf_op jit(solution)/shard_map/all_to_all | solution.py:112
  266.0 5.8 %copy-start.8 = (s32[128,8]{0,1:T(8,128)S(1)}, s32[128,8]{0,1:T(8,128)}, u32[]{:S(2)}) copy-start(s32[128,8]{0,1:T(8,128)} %param.21) | copy-start | bytes 12292
  266.0 6.0 %copy-start.7 = (bf16[2048,128]{1,0:T(8,128)(2,1)S(1)}, bf16[2048,128]{1,0:T(8,128)(2,1)}, u32[]{:S(2)}) copy-start(bf16[2048,128]{1,0:T(8,128)(2,1)} %param.30) | copy-start | bytes 1572868
  266.0 54.3 %all-to-all-start.2 = ((bf16[8,128,2048]{2,1,0:T(8,128)(2,1)}), bf16[8,128,2048]{2,1,0:T(8,128)(2,1)}, u32[]{:S(2)}, u32[]{:S(2)}) async-start(bf16[8,128,2048]{2,1,0:T(8,128)(2,1)} %bitcast.86), calls=%async_computation.2 | async-start | bytes 8388608 | tf_op jit(solution)/shard_map/all_to_all | solution.py:115
  320.3 19.2 %copy-start.1 = (bf16[2048,512]{1,0:T(8,128)(2,1)S(1)}, bf16[2048,512]{1,0:T(8,128)(2,1)}, u32[]{:S(2)}) copy-start(bf16[2048,512]{1,0:T(8,128)(2,1)} %param.25) | copy-start | bytes 6291460
  332.0 6.6 %copy-start.4 = (f32[128,2048]{1,0:T(8,128)S(1)}, f32[128,2048]{1,0:T(8,128)}, u32[]{:S(2)}) copy-start(f32[128,2048]{1,0:T(8,128)} %copy-done.3) | copy-start | bytes 3145732
where the time goes:
time: 342 us; the launch traced here: 340 us
  Pallas kernels  102 us (30%)
  waiting for transfers between devices  78.2 us (23%)
  local copies, waits for them, and re-layouts  60.7 us (18%)
  other arithmetic  51.2 us (15%)
  matrix products  29.9 us (9%)
  starting transfers between devices  16.5 us (5%)
    another operation x3, Pallas kernels  100 us
    all_to_all x1, waiting for transfers between devices, device_step(): lax.all_to_all(expert_out.reshape(ep_size, cap_rows, hidden), 'ep', 0, 0,...  40.9 us
    all_to_all x1, waiting for transfers between devices, device_step(): lax.all_to_all(send_rows, 'ep', 0, 0, tiled=True)  37.4 us
    gather x1, local copies, waits for them, and re-layouts, unpack_rows(): picked = back_rows[flat_slot].reshape(b_dev, top_k, back_rows.shape[1])  11.7 us
    gather x1, local copies, waits for them, and re-layouts, expert_rows(): tok_rows[sort_order]  11.6 us
    gather x1, local copies, waits for them, and re-layouts, expert_rows(): return sorted_out[jnp.argsort(sort_order, stable=True)]  11.6 us
    dot_general x1, matrix products, attend_block(): jnp.dot(attn_out, w_o, preferred_element_type=jnp.float32)  8.49 us
    dot_general x1, matrix products, attend_block(): jnp.dot(normed, w_q, preferred_element_type=jnp.float32)  8.22 us
  transfers between devices with their start and end apart: 3, of which 2 were waited for; matrix products, arithmetic and copies ran while one was open for 20% of the time, Pallas kernels for 1%

commit v1 on v0

v1 whole, which is shorter than its diff:
```python
import functools

import jax
import jax.numpy as jnp
from jax import lax
from jax.experimental import pallas as pl
from jax.experimental.pallas import tpu as pltpu
from jax.sharding import PartitionSpec as P

ROPE_BASE = 1000000.0
NORM_EPS = 1e-6
MESH = pl.DeviceIdType.MESH
F32 = jnp.float32
BF16 = jnp.bfloat16
SEATS = 128
SPLIT = 4


def norm_scale(values, gain_vec):
    return values * lax.rsqrt(jnp.mean(values * values, axis=-1, keepdims=True) + NORM_EPS) * gain_vec.astype(jnp.float32)


def rotate_halves(values, positions):
    half_dim = values.shape[-1] // 2
    freq_vec = ROPE_BASE ** (-jnp.arange(half_dim, dtype=jnp.float32) * 2.0 / values.shape[-1])
    angles = positions.astype(jnp.float32)[:, None, None] * freq_vec
    cosine = jnp.cos(angles)
    sine_val = jnp.sin(angles)
    lo_half = values[..., :half_dim]
    hi_half = values[..., half_dim:]
    return jnp.concatenate([lo_half * cosine - hi_half * sine_val, hi_half * cosine + lo_half * sine_val], axis=-1)


def attend_block(x_in, k_cache, v_cache, cache_len, ln_attn, w_q, w_k, w_v, q_norm, k_norm, w_o):
    n_batch, n_slots, kv_heads, head_dim = k_cache.shape
    q_heads = w_q.shape[1] // head_dim
    resid_in = x_in.astype(jnp.float32)
    normed = norm_scale(resid_in, ln_attn).astype(jnp.bfloat16)
    q_proj = jnp.dot(normed, w_q, preferred_element_type=jnp.float32).reshape(n_batch, q_heads, head_dim)
    k_proj = jnp.dot(normed, w_k, preferred_element_type=jnp.float32).reshape(n_batch, kv_heads, head_dim)
    v_new = jnp.dot(normed, w_v, preferred_element_type=jnp.float32).astype(jnp.bfloat16).reshape(n_batch, kv_heads, head_dim)
    q_rot = rotate_halves(norm_scale(q_proj, q_norm), cache_len).astype(jnp.bfloat16).reshape(n_batch, kv_heads, q_heads // kv_heads, head_dim)
    k_new = rotate_halves(norm_scale(k_proj, k_norm), cache_len).astype(jnp.bfloat16)
    len_col = cache_len[:, None, None, None]
    is_new = lax.broadcasted_iota(jnp.int32, (1, n_slots, 1, 1), 1) == len_col
    k_full = jnp.where(is_new, k_new[:, None], k_cache)
    v_full = jnp.where(is_new, v_new[:, None], v_cache)
    scores = jnp.einsum('bgrd,bsgd->bgrs', q_rot, k_full, preferred_element_type=jnp.float32) * head_dim ** -0.5
    seen = lax.broadcasted_iota(jnp.int32, (1, 1, 1, n_slots), 3) <= len_col
    attn_prob = jax.nn.softmax(jnp.where(seen, scores, -1e30), axis=-1).astype(jnp.bfloat16)
    attn_out = jnp.einsum('bgrs,bsgd->bgrd', attn_prob, v_full, preferred_element_type=jnp.float32).astype(jnp.bfloat16).reshape(n_batch, q_heads * head_dim)
    x_mid = (resid_in + jnp.dot(attn_out, w_o, preferred_element_type=jnp.float32)).astype(jnp.bfloat16)
    return x_mid, k_full, v_full


def route_gate(x_mid, ln_moe, w_router, topk_idx):
    resid_mid = x_mid.astype(jnp.float32)
    h_moe = norm_scale(resid_mid, ln_moe).astype(jnp.bfloat16)
    logits = jnp.dot(h_moe, w_router, preferred_element_type=jnp.float32)
    gate_wts = jax.nn.softmax(jnp.take_along_axis(logits, topk_idx, axis=1), axis=-1)
    return h_moe, gate_wts


def moe_kernel(ep_size, h_ref, x_ref, meta_ref, wg_hbm, wu_hbm, wd_hbm, out_ref, flag_ref,
               xall, mall, perm, keys, keyt, xg, hid, ys, ybuf, yrecv, zsum, recv1, recv2, fin,
               wg, wu, wd, s_w, s_d, s_own, s_fwd, s_pair, r_x, s_meta, r_meta,
               s_y, r_y, s_1, r_1, s_2, r_2, s_f, r_f):
    b_dev, hidden = h_ref.shape
    e_local, _, ff = wg_hbm.shape
    n_chip = ep_size // 2
    half = b_dev // 2
    wide = hidden // SPLIT
    side = wide // 2
    n_a, n_b = wg.shape[0], wd.shape[0]
    per = wd.shape[1]
    groups = e_local // per
    me = lax.axis_index('ep')
    chip, core = me // 2, me % 2
    right = lax.rem(chip + 1, n_chip)
    left = lax.rem(chip + n_chip - 1, n_chip)
    far = lax.rem(chip + 2, n_chip)
    dev_r, dev_l, mate = right * 2 + core, left * 2 + core, chip * 2 + 1 - core

    def load_a(e):
        slot = lax.rem(e, n_a)
        return (pltpu.make_async_copy(wg_hbm.at[e], wg.at[slot], s_w.at[0, slot]),
                pltpu.make_async_copy(wu_hbm.at[e], wu.at[slot], s_w.at[1, slot]))

    def load_b(i):
        slot = lax.rem(i, n_b)
        q, g = i // groups, lax.rem(i, groups)
        cols = pl.ds(pl.multiple_of(q * wide, wide), wide)
        return pltpu.make_async_copy(wd_hbm.at[pl.ds(g * per, per), :, cols], wd.at[slot], s_d.at[slot])

    for e in range(n_a):
        for c in load_a(e):
            c.start()
    for i in range(n_b):
        load_b(i).start()

    barrier = pltpu.get_barrier_semaphore()
    for k in range(1, ep_size):
        pl.semaphore_signal(barrier, inc=1, device_id={'ep': lax.rem(me + k, ep_size)}, device_id_type=MESH)
    pl.semaphore_wait(barrier, ep_size - 1)

    def part(h):
        return pl.ds(h * half, half)

    def send_own(h, target, sem):
        return pltpu.make_async_remote_copy(h_ref.at[part(h)], xall.at[me, part(h)], sem, r_x.at[me, h],
                                            device_id={'ep': target}, device_id_type=MESH)

    def forward(src, h, target, sem):
        return pltpu.make_async_remote_copy(xall.at[src, part(h)], xall.at[src, part(h)], sem, r_x.at[src, h],
                                            device_id={'ep': target}, device_id_type=MESH)

    def send_meta(k):
        return pltpu.make_async_remote_copy(meta_ref, mall.at[me], s_meta.at[k - 1], r_meta.at[me],
                                            device_id={'ep': lax.rem(me + k, ep_size)}, device_id_type=MESH)

    started = []

    def go(copy):
        copy.start()
        started.append(copy)

    for k in range(1, ep_size):
        go(send_meta(k))
    go(send_own(0, dev_r, s_own.at[0]))
    go(send_own(1, dev_l, s_own.at[1]))
    go(send_own(1, dev_r, s_own.at[2]))
    go(send_own(0, dev_l, s_own.at[3]))
    go(send_own(0, mate, s_own.at[4]))
    go(send_own(1, mate, s_own.at[5]))
    xall[me] = h_ref[...]
    mall[me] = meta_ref[...]

    forward(dev_l, 0, dev_r, s_fwd.at[0]).wait_recv()
    go(forward(dev_l, 0, dev_r, s_fwd.at[0]))
    go(forward(dev_l, 0, mate, s_pair.at[0]))
    forward(dev_r, 1, dev_l, s_fwd.at[1]).wait_recv()
    go(forward(dev_r, 1, dev_l, s_fwd.at[1]))
    go(forward(dev_r, 1, mate, s_pair.at[1]))

    for k in range(1, ep_size):
        src = lax.rem(me + k, ep_size)
        pltpu.make_async_remote_copy(meta_ref, mall.at[src], s_meta.at[k - 1], r_meta.at[src],
                                     device_id={'ep': src}, device_id_type=MESH).wait_recv()
    lower = lax.broadcasted_iota(jnp.int32, (b_dev, b_dev), 0) < lax.broadcasted_iota(jnp.int32, (b_dev, b_dev), 1)
    before = jnp.where(lower, 1.0, 0.0).astype(BF16)
    ids16 = lax.broadcasted_iota(jnp.int32, (e_local, b_dev), 0).astype(F32)
    keys[...] = jnp.zeros_like(keys)
    counts = jnp.zeros((e_local, 1), F32)
    for src in range(ep_size):
        row = mall[src, pl.ds(me, 1), :]
        hot = jnp.where(ids16 == row, 1.0, 0.0)
        ranks = jnp.dot(hot.astype(BF16), before, preferred_element_type=F32) + counts
        rank = jnp.sum(hot * ranks, axis=0, keepdims=True)
        keys[pl.ds(src, 1), :] = row * SEATS + rank
        keys[pl.ds(ep_size + src, 1), :] = mall[src, pl.ds(ep_size + me, 1), :]
        keys[pl.ds(2 * ep_size + src, 1), :] = mall[src, pl.ds(ep_size + mate, 1), :]
        counts = counts + jnp.sum(hot, axis=1, keepdims=True)
    keyt[...] = jnp.transpose(keys[...])
    most = jnp.zeros((e_local, 1), F32)
    for dev in range(ep_size):
        total = jnp.zeros((e_local, 1), F32)
        for src in range(ep_size):
            hot = jnp.where(ids16 == mall[src, pl.ds(dev, 1), :], 1.0, 0.0)
            total = total + jnp.sum(hot, axis=1, keepdims=True)
        most = jnp.maximum(most, total)
    flag_ref[...] = jnp.broadcast_to(jnp.max(most, axis=0, keepdims=True), flag_ref.shape)

    seat_cols = lax.broadcasted_iota(jnp.int32, (b_dev, 4 * SEATS), 1).astype(F32)
    for b in range(ep_size):
        col = keyt[:, b:b + 1]

        @pl.loop(0, e_local // 4)
        def _(j):
            base = (j * (4 * SEATS)).astype(F32)
            hot = jnp.where(seat_cols + base == col, 1.0, 0.0).astype(BF16)
            perm[b * b_dev:(b + 1) * b_dev, pl.ds(pl.multiple_of(j * (4 * SEATS), 4 * SEATS), 4 * SEATS)] = hot

    for src, h, sem in ((dev_l, 1, 2), (dev_r, 0, 3)):
        forward(src, h, mate, s_pair.at[sem]).wait_recv()
        go(forward(src, h, mate, s_pair.at[sem]))
    dev_f = far * 2 + core
    for h in range(2):
        forward(dev_f, h, mate, s_pair.at[4 + h]).wait_recv()
        go(forward(dev_f, h, mate, s_pair.at[4 + h]))
    for k in range(n_chip):
        src = lax.rem(chip + k, n_chip) * 2 + 1 - core
        for h in range(2):
            forward(src, h, mate, s_pair.at[h]).wait_recv()

    seat_rows = lax.broadcasted_iota(jnp.int32, (SEATS, b_dev), 0).astype(F32)

    @pl.loop(0, e_local)
    def _(e):
        slot = lax.rem(e, n_a)
        base = (e * SEATS).astype(F32)
        pick = jnp.concatenate(
            [jnp.where(keys[b:b + 1, :] == seat_rows + base, 1.0, 0.0).astype(BF16) for b in range(ep_size)], axis=1)
        for n in range(4):
            cols = slice(n * (hidden // 4), (n + 1) * (hidden // 4))
            rows = xall[:, :, cols].reshape(ep_size * b_dev, hidden // 4)
            xg[:, cols] = jnp.dot(pick, rows, preferred_element_type=F32).astype(BF16)
        for c in load_a(e):
            c.wait()
        for n in range(ff // 256):
            cols = slice(n * 256, (n + 1) * 256)
            gate = jnp.dot(xg[...], wg[slot, :, cols], preferred_element_type=F32)
            up = jnp.dot(xg[...], wu[slot, :, cols], preferred_element_type=F32)
            hid[e, :, cols] = (gate * jax.nn.sigmoid(gate) * up).astype(BF16)

        @pl.when(e + n_a < e_local)
        def _():
            for c in load_a(e + n_a):
                c.start()

    def send_y(q):
        return pltpu.make_async_remote_copy(ybuf.at[q, 1 - core], yrecv.at[q], s_y.at[q], r_y.at[q],
                                            device_id={'ep': mate}, device_id_type=MESH)

    def send_1(q, d):
        block = far * 2 + d
        return pltpu.make_async_remote_copy(zsum.at[q, block], recv1.at[d, q], s_1.at[d, q], r_1.at[d, q],
                                            device_id={'ep': dev_l if d else dev_r}, device_id_type=MESH)

    def send_2(q, d):
        block = (left if d else right) * 2
        return pltpu.make_async_remote_copy(zsum.at[q, pl.ds(block, 2)], recv2.at[d, q], s_2.at[d, q], r_2.at[d, q],
                                            device_id={'ep': dev_l if d else dev_r}, device_id_type=MESH)

    def send_f(q):
        return pltpu.make_async_remote_copy(zsum.at[q, mate], fin.at[q], s_f.at[q], r_f.at[q],
                                            device_id={'ep': mate}, device_id_type=MESH)

    def relay(q):
        for d in range(2):
            send_1(q, d).wait_recv()
            block = (left if d else right) * 2 + d
            zsum[q, block] = zsum[q, block] + recv1[d, q]
            send_2(q, d).start()

    @pl.loop(0, SPLIT)
    def _(q):
        @pl.loop(0, groups)
        def _(g):
            i = q * groups + g
            slot = lax.rem(i, n_b)
            load_b(i).wait()
            for j in range(per):
                e = g * per + j
                ys[pl.ds(pl.multiple_of(e * SEATS, SEATS), SEATS), :] = jnp.dot(
                    hid[e], wd[slot, j], preferred_element_type=F32).astype(BF16)

            @pl.when(i + n_b < SPLIT * groups)
            def _():
                load_b(i + n_b).start()

        @pl.loop(0, ep_size // 2)
        def _(m):
            rows = pl.ds(pl.multiple_of(m * (2 * b_dev), 2 * b_dev), 2 * b_dev)
            for h in range(2):
                part_y = jnp.dot(perm[rows, :], ys[:, h * side:(h + 1) * side], preferred_element_type=F32)
                ybuf[q, h, pl.ds(2 * m, 2)] = part_y.astype(BF16).reshape(2, b_dev, side)

        send_y(q).start()

        @pl.when(q > 0)
        def _():
            relay(q - 1)

        send_y(q).wait_recv()
        for b in range(ep_size):
            zsum[q, b] = (keyt[:, ep_size + b:ep_size + b + 1] * ybuf[q, core, b].astype(F32)
                          + keyt[:, 2 * ep_size + b:2 * ep_size + b + 1] * yrecv[q, b].astype(F32))
        send_1(q, 0).start()
        send_1(q, 1).start()

    relay(SPLIT - 1)

    def columns(q, which):
        return pl.ds(pl.multiple_of(q * wide + which * side, side), side)

    @pl.loop(0, SPLIT)
    def _(q):
        send_2(q, 0).wait_recv()
        send_2(q, 1).wait_recv()
        zsum[q, mate] = zsum[q, mate] + recv2[0, q, 1 - core] + recv2[1, q, 1 - core]
        send_f(q).start()
        mine = zsum[q, me] + recv2[0, q, core] + recv2[1, q, core]
        cols = columns(q, core)
        out_ref[:, cols] = (x_ref[:, cols].astype(F32) + mine).astype(BF16)

    @pl.loop(0, SPLIT)
    def _(q):
        send_f(q).wait_recv()
        cols = columns(q, 1 - core)
        out_ref[:, cols] = (x_ref[:, cols].astype(F32) + fin[q]).astype(BF16)

    for copy in started:
        copy.wait_send()

    @pl.loop(0, SPLIT)
    def _(q):
        send_y(q).wait_send()
        send_f(q).wait_send()
        for d in range(2):
            send_1(q, d).wait_send()
            send_2(q, d).wait_send()


def moe_block(ep_size, h_moe, x_mid, meta, w_gate, w_up, w_down):
    b_dev, hidden = h_moe.shape
    e_local, _, ff = w_gate.shape
    wide, side = hidden // SPLIT, hidden // SPLIT // 2
    n_a, n_b, per = 3, 4, 4
    vmem, dma = pltpu.VMEM, pltpu.SemaphoreType.DMA
    tokens = ep_size * b_dev
    return pl.pallas_call(
        functools.partial(moe_kernel, ep_size),
        out_shape=(jax.ShapeDtypeStruct((b_dev, hidden), BF16), jax.ShapeDtypeStruct((8, 128), F32)),
        in_specs=[pl.BlockSpec(memory_space=pltpu.VMEM)] * 3 + [pl.BlockSpec(memory_space=pl.ANY)] * 3,
        out_specs=(pl.BlockSpec(memory_space=pltpu.VMEM), pl.BlockSpec(memory_space=pltpu.VMEM)),
        scratch_shapes=[
            vmem((ep_size, b_dev, hidden), BF16), vmem((ep_size, 2 * ep_size, b_dev), F32),
            vmem((tokens, e_local * SEATS), BF16), vmem((b_dev, b_dev), F32), vmem((b_dev, b_dev), F32),
            vmem((SEATS, hidden), BF16), vmem((e_local, SEATS, ff), BF16), vmem((e_local * SEATS, wide), BF16),
            vmem((SPLIT, 2, ep_size, b_dev, side), BF16), vmem((SPLIT, ep_size, b_dev, side), BF16),
            vmem((SPLIT, ep_size, b_dev, side), F32), vmem((2, SPLIT, b_dev, side), F32),
            vmem((2, SPLIT, 2, b_dev, side), F32), vmem((SPLIT, b_dev, side), F32),
            vmem((n_a, hidden, ff), BF16), vmem((n_a, hidden, ff), BF16), vmem((n_b, per, ff, wide), BF16),
            dma((2, n_a)), dma((n_b,)), dma((6,)), dma((2,)), dma((6,)), dma((ep_size, 2)),
            dma((ep_size - 1,)), dma((ep_size,)),
            dma((SPLIT,)), dma((SPLIT,)), dma((2, SPLIT)), dma((2, SPLIT)), dma((2, SPLIT)), dma((2, SPLIT)),
            dma((SPLIT,)), dma((SPLIT,)),
        ],
        compiler_params=pltpu.CompilerParams(collective_id=0, has_side_effects=True, vmem_limit_bytes=67043328),
        name='moe',
    )(h_moe, x_mid, meta, w_gate, w_up, w_down)


def moe_general(ep_size, h_moe, x_mid, topk_idx, gate_wts, w_gate, w_up, w_down):
    b_dev, hidden = h_moe.shape
    e_local = w_gate.shape[0]
    owner = topk_idx // e_local
    hot = owner[:, None, :] == jnp.arange(ep_size)[None, :, None]
    local = jnp.sum(jnp.where(hot, (topk_idx % e_local)[:, None, :], 0), axis=2).T
    wts = jnp.sum(jnp.where(hot, gate_wts[:, None, :], 0.0), axis=2)
    rows = lax.all_to_all(jnp.broadcast_to(h_moe[None], (ep_size, b_dev, hidden)), 'ep', 0, 0, tiled=True)
    rows = rows.reshape(ep_size * b_dev, hidden)
    ids = lax.all_to_all(local[:, None, :], 'ep', 0, 0, tiled=True).reshape(ep_size * b_dev)

    def one(e, done):
        gate = jnp.dot(rows, w_gate[e], preferred_element_type=F32)
        up = jnp.dot(rows, w_up[e], preferred_element_type=F32)
        act = (jax.nn.silu(gate) * up).astype(BF16)
        y = jnp.dot(act, w_down[e], preferred_element_type=F32).astype(BF16)
        return jnp.where((ids == e)[:, None], y, done)

    y = lax.fori_loop(0, e_local, one, jnp.zeros(rows.shape, BF16))
    back = lax.all_to_all(y.reshape(ep_size, b_dev, hidden), 'ep', 0, 0, tiled=True)
    total = jnp.sum(back.astype(F32) * wts.T[:, :, None], axis=0)
    return (x_mid.astype(F32) + total).astype(BF16)


def solution(mesh):
    ep_size = mesh.shape['ep']
    row_spec = P(('dp', 'ep'))
    replicated = P()
    expert_spec = P('ep')
    in_specs = (row_spec,) * 5 + (replicated,) * 9 + (expert_spec,) * 3
    out_specs = (row_spec, row_spec, row_spec)

    def device_step(x_in, k_cache, v_cache, cache_len, topk_idx, ln_attn, w_q, w_k, w_v, q_norm, k_norm, w_o, ln_moe, w_router, w_gate, w_up, w_down):
        x_mid, k_full, v_full = attend_block(x_in, k_cache, v_cache, cache_len, ln_attn, w_q, w_k, w_v, q_norm, k_norm, w_o)
        h_moe, gate_wts = route_gate(x_mid, ln_moe, w_router, topk_idx)
        e_local = w_gate.shape[0]
        owner = topk_idx // e_local
        hot = owner[:, None, :] == jnp.arange(ep_size)[None, :, None]
        local = jnp.sum(jnp.where(hot, (topk_idx % e_local)[:, None, :], 0), axis=2).astype(F32)
        wts = jnp.sum(jnp.where(hot, gate_wts[:, None, :], 0.0), axis=2)
        meta = jnp.concatenate([local, wts], axis=1).T
        fast, most = moe_block(ep_size, h_moe, x_mid, meta, w_gate, w_up, w_down)
        x_out = lax.cond(most[0, 0] > SEATS,
                         lambda: moe_general(ep_size, h_moe, x_mid, topk_idx, gate_wts, w_gate, w_up, w_down),
                         lambda: fast)
        return x_out, k_full, v_full

    return jax.shard_map(device_step, mesh=mesh, in_specs=in_specs, out_specs=out_specs, check_vma=False)
```

time: 342 us -> 163 us (0.48)
  waiting for transfers between devices: 78.2 us -> 0 us
  local copies, waits for them, and re-layouts: 60.7 us -> 15.2 us
  other arithmetic: 51.2 us -> 14.8 us
  starting transfers between devices: 16.5 us -> 0 us
  matrix products: 29.9 us -> 26 us
    pallas_call x0 -> x1, Pallas kernels: none -> 105 us  [moe_block(): pl.pallas_call(functools.partial(moe_kernel, ep_size), out_shape=(jax.Sha...]
    another operation x3 -> x0, Pallas kernels: 100 us -> none
    all_to_all x3 -> x0, waiting for transfers between devices: 78.2 us -> none  [the longest x1 40.9 us: device_step(): lax.all_to_all(expert_out.reshape(ep_size, cap_rows, hidden), 'ep', 0, 0,...]
    gather x6 -> x0, local copies, waits for them, and re-layouts: 49.9 us -> none  [the longest x1 11.7 us: unpack_rows(): picked = back_rows[flat_slot].reshape(b_dev, top_k, back_rows.shape[1])]
    all_to_all x3 -> x0, starting transfers between devices: 16.5 us -> none  [the longest x1 6.01 us: device_step(): lax.all_to_all(send_ids, 'ep', 0, 0, tiled=True).reshape(ep_size * cap_rows)]
    sort x3 -> x0, other arithmetic: 13.1 us -> none  [the longest x1 4.38 us: pack_rows(): sort_order = jnp.argsort(dest_dev, stable=True)]
    convert_element_type x4 -> x1, other arithmetic: 11.8 us -> 0.01 us  [device_step(): jnp.sum(jnp.where(hot, (topk_idx % e_local)[:, None, :], 0), axis=2)]
    reduce_sum x3 -> x2, other arithmetic: 7.35 us -> 0.03 us  [the longest x1 0.02 us: device_step(): wts = jnp.sum(jnp.where(hot, gate_wts[:, None, :], 0.0), axis=2)]
  transfers between devices with their start and end apart: 3 -> 0, of which waited for: 2 -> 0; matrix products, arithmetic and copies ran while one was open for 20% -> 0% of each run, Pallas kernels for 1% -> 0%
where the time goes in v1:
time: 163 us
  Pallas kernels  105 us (64%)
  matrix products  26 us (16%)
  local copies, waits for them, and re-layouts  15.2 us (9%)
  other arithmetic  14.8 us (9%)
  between operations  1.72 us (1%)
    pallas_call x1, Pallas kernels, moe_block(): pl.pallas_call(functools.partial(moe_kernel, ep_size), out_shape=(jax.Sha...  105 us
    dot_general x1, matrix products, attend_block(): jnp.dot(attn_out, w_o, preferred_element_type=jnp.float32)  8.56 us
    select_n x1, other arithmetic, attend_block(): k_full = jnp.where(is_new, k_new[:, None], k_cache)  8.08 us
    gather x5, local copies, waits for them, and re-layouts, route_gate(): jnp.take_along_axis(logits, topk_idx, axis=1)  7.12 us
    unnamed x24, local copies, waits for them, and re-layouts  6.7 us
    sub x1, matrix products, attend_block(): jax.nn.softmax(jnp.where(seen, scores, -1e+30), axis=-1)  6.17 us
    dot_general x1, matrix products, attend_block(): jnp.einsum('bgrs,bsgd->bgrd', attn_prob, v_full, preferred_element_type=j...  4.09 us

profile of v1, /device:TPU:113, one launch (start us, length us, event | category | flops | bytes accessed | tf_op | source)
XLA Modules:
  0.0 162.7 jit_solution(16438052536218012856)
XLA Ops:
  0.6 0.0 copy-start.11
  0.6 0.0 copy-start.10
  0.7 0.7 convert_element_type.80
  1.4 1.3 fusion.35
  2.7 2.3 %fusion.58 = f32[128,512]{1,0:T(8,128)S(1)} fusion(bf16[2048,512]{1,0:T(8,128)(2,1)} %param.28, bf16[128,2048]{1,0:T(8,128)(2,1)} %param.21, f32[2048]{0:T(1024)S(1)} %convert_element_type.80, f32[128]{0:T(128)S(1)} %add_rsqrt_fusion.3), kind=kOutput, calls=%fused_computation.112 | convolution fusion | flops 269484032 | bytes 2892288 | tf_op jit(solution)/shard_map/dot_general | solution.py:40
  4.9 0.1 reshape.234
  5.0 0.2 multiply_reduce_fusion.2
  5.3 0.0 copy-done.11
  5.3 0.2 multiply_multiply_fusion.1
  5.5 0.0 copy-done.10
  5.5 0.3 multiply_cosine_fusion
  5.8 0.3 subtract_convert_fusion.1
  6.1 0.2 pad_maximum_fusion
  6.3 0.0 copy-done.1
  6.3 2.1 %convolution_convert_fusion = bf16[128,512]{1,0:T(8,128)(2,1)S(1)} fusion(bf16[2048,512]{1,0:T(8,128)(2,1)} %param.29, bf16[128,2048]{1,0:T(8,128)(2,1)S(1)} %copy-done.1, f32[2048]{0:T(1024)S(1)} %convert_element_type.80, f32[128]{0:T(128)S(1)} %add_rsqrt_fusion.3), kind=kOutput, calls=%fused_computation.58 | convolution fusion | flops 269549568 | bytes 2761216 | tf_op jit(solution)/shard_map/dot_general | solution.py:41
  8.5 0.1 iota_compare_fusion.2
  8.6 0.0 copy-start
  8.6 8.1 %broadcast_select_fusion.1 = (bf16[128,32,4,128]{3,2,1,0:T(4,128)(2,1)}, bf16[128,32,4,128]{3,2,1,0:T(4,128)(2,1)}) fusion(bf16[128,32,4,128]{3,2,1,0:T(4,128)(2,1)} %param.22, pred[128,32]{1,0:T(8,128)(4,1)S(1)} %get-tuple-element.228, bf16[128,4,128]{2,1,0:T(4,128)(2,1)S(1)} %pad_maximum_fusion, bf16[128,32,4,128]{3,2,1,0:T(4,128)(2,1)} %param.23, ...), kind=kLoop, calls=%fused_computation.41 | loop fusion | flops 4194304 | bytes 17043456 | tf_op jit(solution)/shard_map/jit(_where)/select_n | solution.py:46
  16.7 3.1 %copy-done = bf16[2048,4096]{1,0:T(8,128)(2,1)S(1)} copy-done((bf16[2048,4096]{1,0:T(8,128)(2,1)S(1)}, bf16[2048,4096]{1,0:T(8,128)(2,1)}, u32[]{:S(2)}) %copy-start) | copy-done | bytes 16777240
  19.7 2.6 %convolution_bitcast_fusion = f32[16,8,32,128]{3,1,2,0:T(8,128)S(1)} fusion(bf16[2048,4096]{1,0:T(8,128)(2,1)S(1)} %copy-done, bf16[128,2048]{1,0:T(8,128)(2,1)S(1)} %copy-done.1, f32[2048]{0:T(1024)S(1)} %convert_element_type.80, f32[128]{0:T(128)S(1)} %add_rsqrt_fusion.3), kind=kOutput, calls=%fused_computation.52 | convolution fusion | flops 2148532224 | bytes 19407360 | tf_op jit(solution)/shard_map/dot_general | solution.py:39
  22.3 0.0 copy-start.12
  22.3 0.4 copy.81
  22.7 0.6 multiply_reduce_fusion.1
  23.3 0.0 copy-done.12
  23.4 1.1 multiply_multiply_fusion
  24.4 0.8 fusion.38
  25.2 6.2 %fusion.61 = (f32[128,4,8]{2,1,0:T(4,128)S(1)}, f32[128,4,8,32]{3,2,1,0:T(8,128)}) fusion(pred[128,32]{1,0:T(8,128)(4,1)S(1)} %get-tuple-element.227, bf16[128,32,4,128]{3,2,1,0:T(4,128)(2,1)} %get-tuple-element.307, bf16[128,4,8,64]{3,2,1,0:T(8,128)(2,1)S(1)} %get-tuple-element.218, bf16[128,4,8,64]{3,2,1,0:T(8,128)(2,1)S(1)} %get-tuple-element.217), kind=kOutput, calls=%fused_computation.113 | convolution fusion | flops 36175904 | bytes 5787648 | tf_op jit(solution)/shard_map/sub | solution.py:50
  31.4 4.1 %fusion.29 = bf16[128,4,8,128]{3,2,1,0:T(8,128)(2,1)S(1)} fusion(bf16[128,32,4,128]{3,2,1,0:T(4,128)(2,1)} %get-tuple-element.308, f32[128,4,8,32]{3,2,1,0:T(8,128)} %get-tuple-element.230, f32[128,4,8]{2,1,0:T(4,128)S(1)} %get-tuple-element.229), kind=kOutput, calls=%fused_computation.55 | convolution fusion | flops 34340864 | bytes 5783552 | tf_op jit(solution)/shard_map/bgrs,bsgd->bgrd/dot_general | solution.py:51
  35.5 0.0 copy-start.9
  35.5 0.0 copy-start.5
  35.5 0.0 copy-start.6
  35.5 8.6 %fusion.32 = (f32[128]{0:T(128)S(1)}, bf16[128,2048]{1,0:T(8,128)(2,1)S(1)}) fusion(bf16[4096,2048]{1,0:T(8,128)(2,1)} %param.32, bf16[16,8,32,128]{3,2,1,0:T(8,128)(2,1)S(1)} %bitcast.89, bf16[128,2048]{1,0:T(8,128)(2,1)S(1)} %copy-done.1), kind=kOutput, calls=%fused_computation.59 | convolution fusion | flops 2149056512 | bytes 18874880 | tf_op jit(solution)/shard_map/dot_general | solution.py:52
  44.1 0.0 copy-start.3
  44.1 0.0 copy-done.9
  44.1 0.2 fusion.34.h_ref
  44.3 0.0 copy-start.2
  44.3 0.8 copy-done.2
  45.1 0.0 copy-done.5
  45.1 0.3 fusion.70
  45.5 0.1 copy.79
  45.6 0.1 reshape.238
  45.7 6.8 %gather_fusion = f32[1024]{0:T(1024)S(1)} fusion(f32[128,128]{1,0:T(8,128)S(1)} %fusion.70, s32[1024]{0:T(1024)S(1)} %reshape.238), kind=kCustom, calls=%fused_computation | custom fusion | bytes 16384 | tf_op jit(solution)/shard_map/jit(take_along_axis)/gather | solution.py:60
  52.5 0.1 reshape.241
  52.8 0.5 copy-done.7
  53.3 0.6 maximum_bitcast_fusion.meta_ref
  53.9 104.9 %moe.1 = (bf16[128,2048]{1,0:T(8,128)(2,1)}, f32[8,128]{1,0:T(8,128)}) custom-call(bf16[128,2048]{1,0:T(8,128)(2,1)} %copy-done.2, bf16[128,2048]{1,0:T(8,128)(2,1)} %copy-done.3, f32[16,128]{1,0:T(8,128)} %maximum_bitcast_fusion.meta_ref, bf16[16,2048,768]{2,1,0:T(8,128)(2,1)} %wg_hbm.1, bf16[16,2048,768]{2,1,0:T(8,128)(2,1)} %wu_hbm.1, ...), custom_call_target="tpu_custom_call" | custom-call | tf_op jit(solution)/shard_map/moe/pallas_call | solution.py:321
  158.8 1.3 slice.19
  160.8 1.9 %copy.109 = bf16[128,2048]{1,0:T(8,128)(2,1)} copy(bf16[128,2048]{1,0:T(8,128)(2,1)} %get-tuple-element.309) | data formatting | bytes 1048576
  (24 shorter events, 0.3 us)
Async XLA Ops:
  0.6 4.6 %copy-start.11 = (bf16[128]{0:T(256)(128)(2,1)S(1)}, bf16[128]{0:T(256)(128)(2,1)}, u32[]{:S(2)}) copy-start(bf16[128]{0:T(256)(128)(2,1)} %param.31) | copy-start | bytes 772
  0.6 4.9 %copy-start.10 = (s32[128]{0:T(128)S(1)}, s32[128]{0:T(128)}, u32[]{:S(2)}) copy-start(s32[128]{0:T(128)} %param.24) | copy-start | bytes 1540
  1.4 5.0 %copy-start.1 = (bf16[128,2048]{1,0:T(8,128)(2,1)S(1)}, bf16[128,2048]{1,0:T(8,128)(2,1)}, u32[]{:S(2)}) copy-start(bf16[128,2048]{1,0:T(8,128)(2,1)} %param.21) | copy-start | bytes 1572868
  8.6 11.2 %copy-start = (bf16[2048,4096]{1,0:T(8,128)(2,1)S(1)}, bf16[2048,4096]{1,0:T(8,128)(2,1)}, u32[]{:S(2)}) copy-start(bf16[2048,4096]{1,0:T(8,128)(2,1)} %param.27) | copy-start | bytes 50331652
  22.3 1.0 copy-start.12
  35.5 8.6 %copy-start.9 = (bf16[2048]{0:T(1024)(128)(2,1)S(1)}, bf16[2048]{0:T(1024)(128)(2,1)}, u32[]{:S(2)}) copy-start(bf16[2048]{0:T(1024)(128)(2,1)} %param.33) | copy-start | bytes 12292
  35.5 9.6 %copy-start.5 = (bf16[2048,128]{1,0:T(8,128)(2,1)S(1)}, bf16[2048,128]{1,0:T(8,128)(2,1)}, u32[]{:S(2)}) copy-start(bf16[2048,128]{1,0:T(8,128)(2,1)} %param.34) | copy-start | bytes 1572868
  35.5 9.9 %copy-start.6 = (s32[128,8]{0,1:T(8,128)S(1)}, s32[128,8]{0,1:T(8,128)}, u32[]{:S(2)}) copy-start(s32[128,8]{0,1:T(8,128)} %param.25) | copy-start | bytes 12292
  44.1 1.3 copy-start.3
  44.3 0.8 copy-start.2
  52.7 0.6 copy-start.7

commit v2 on v1

--- a/solution.py
+++ b/solution.py
@@ -16,49 +16,179 @@
 SPLIT = 4
 
 
-def norm_scale(values, gain_vec):
-    return values * lax.rsqrt(jnp.mean(values * values, axis=-1, keepdims=True) + NORM_EPS) * gain_vec.astype(jnp.float32)
-
-
-def rotate_halves(values, positions):
-    half_dim = values.shape[-1] // 2
-    freq_vec = ROPE_BASE ** (-jnp.arange(half_dim, dtype=jnp.float32) * 2.0 / values.shape[-1])
-    angles = positions.astype(jnp.float32)[:, None, None] * freq_vec
-    cosine = jnp.cos(angles)
-    sine_val = jnp.sin(angles)
-    lo_half = values[..., :half_dim]
-    hi_half = values[..., half_dim:]
-    return jnp.concatenate([lo_half * cosine - hi_half * sine_val, hi_half * cosine + lo_half * sine_val], axis=-1)
-
-
-def attend_block(x_in, k_cache, v_cache, cache_len, ln_attn, w_q, w_k, w_v, q_norm, k_norm, w_o):
-    n_batch, n_slots, kv_heads, head_dim = k_cache.shape
-    q_heads = w_q.shape[1] // head_dim
-    resid_in = x_in.astype(jnp.float32)
-    normed = norm_scale(resid_in, ln_attn).astype(jnp.bfloat16)
-    q_proj = jnp.dot(normed, w_q, preferred_element_type=jnp.float32).reshape(n_batch, q_heads, head_dim)
-    k_proj = jnp.dot(normed, w_k, preferred_element_type=jnp.float32).reshape(n_batch, kv_heads, head_dim)
-    v_new = jnp.dot(normed, w_v, preferred_element_type=jnp.float32).astype(jnp.bfloat16).reshape(n_batch, kv_heads, head_dim)
-    q_rot = rotate_halves(norm_scale(q_proj, q_norm), cache_len).astype(jnp.bfloat16).reshape(n_batch, kv_heads, q_heads // kv_heads, head_dim)
-    k_new = rotate_halves(norm_scale(k_proj, k_norm), cache_len).astype(jnp.bfloat16)
-    len_col = cache_len[:, None, None, None]
-    is_new = lax.broadcasted_iota(jnp.int32, (1, n_slots, 1, 1), 1) == len_col
-    k_full = jnp.where(is_new, k_new[:, None], k_cache)
-    v_full = jnp.where(is_new, v_new[:, None], v_cache)
-    scores = jnp.einsum('bgrd,bsgd->bgrs', q_rot, k_full, preferred_element_type=jnp.float32) * head_dim ** -0.5
-    seen = lax.broadcasted_iota(jnp.int32, (1, 1, 1, n_slots), 3) <= len_col
-    attn_prob = jax.nn.softmax(jnp.where(seen, scores, -1e30), axis=-1).astype(jnp.bfloat16)
-    attn_out = jnp.einsum('bgrs,bsgd->bgrd', attn_prob, v_full, preferred_element_type=jnp.float32).astype(jnp.bfloat16).reshape(n_batch, q_heads * head_dim)
-    x_mid = (resid_in + jnp.dot(attn_out, w_o, preferred_element_type=jnp.float32)).astype(jnp.bfloat16)
-    return x_mid, k_full, v_full
-
-
-def route_gate(x_mid, ln_moe, w_router, topk_idx):
-    resid_mid = x_mid.astype(jnp.float32)
-    h_moe = norm_scale(resid_mid, ln_moe).astype(jnp.bfloat16)
-    logits = jnp.dot(h_moe, w_router, preferred_element_type=jnp.float32)
-    gate_wts = jax.nn.softmax(jnp.take_along_axis(logits, topk_idx, axis=1), axis=-1)
-    return h_moe, gate_wts
+def rms(values, gain):
+    return values * lax.rsqrt(jnp.mean(values * values, axis=-1, keepdims=True) + NORM_EPS) * gain
+
+
+def attend_kernel(ep_size, len_ref, x_ref, cos_ref, sin_ref, idx_ref, lna_ref, qn_ref, kn_ref, lnm_ref,
+                  wq_hbm, wk_hbm, wv_hbm, wo_hbm, wr_hbm, kc_hbm, vc_hbm,
+                  xmid_ref, h_ref, meta_ref, ko_hbm, vo_hbm,
+                  wq, wk, wv, wo, wr, kbuf, vbuf, qs, os, knew, vnew, hn, att,
+                  s_q, s_kv, s_o, s_c, s_out):
+    b_dev, hidden = x_ref.shape
+    _, lanes, dim = kbuf.shape
+    q_width = wq.shape[1]
+    q_heads, kv_heads = q_width // dim, wk.shape[1] // dim
+    n_q, n_o = s_q.shape[0], s_o.shape[0]
+    n_blk = s_c.shape[1]
+    blk = b_dev // n_blk
+    qc, oc = q_width // n_q, hidden // n_o
+    rep = q_heads // kv_heads
+
+    def copy_q(i):
+        cols = pl.ds(pl.multiple_of(i * qc, qc), qc)
+        return pltpu.make_async_copy(wq_hbm.at[:, cols], wq.at[:, cols], s_q.at[i])
+
+    def copy_o(i):
+        cols = pl.ds(pl.multiple_of(i * oc, oc), oc)
+        return pltpu.make_async_copy(wo_hbm.at[:, cols], wo.at[:, cols], s_o.at[i])
+
+    def copy_in(b):
+        rows = pl.ds(b * blk, blk)
+        return (pltpu.make_async_copy(kc_hbm.at[rows], kbuf.at[rows], s_c.at[0, b]),
+                pltpu.make_async_copy(vc_hbm.at[rows], vbuf.at[rows], s_c.at[1, b]))
+
+    def copy_out(b):
+        rows = pl.ds(b * blk, blk)
+        return (pltpu.make_async_copy(kbuf.at[rows], ko_hbm.at[rows], s_out.at[0, b]),
+                pltpu.make_async_copy(vbuf.at[rows], vo_hbm.at[rows], s_out.at[1, b]))
+
+    small = (pltpu.make_async_copy(wk_hbm, wk, s_kv.at[0]), pltpu.make_async_copy(wv_hbm, wv, s_kv.at[1]),
+             pltpu.make_async_copy(wr_hbm, wr, s_kv.at[2]))
+    for c in small[:2]:
+        c.start()
+    for i in range(n_q):
+        copy_q(i).start()
+    for b in range(n_blk):
+        for c in copy_in(b):
+            c.start()
+    for i in range(n_o):
+        copy_o(i).start()
+    small[2].start()
+
+    x = x_ref[...].astype(F32)
+    hn[...] = rms(x, lna_ref[...].astype(F32)).astype(BF16)
+    cos, sin = cos_ref[...], sin_ref[...]
+
+    def turned(values, gain):
+        normed = rms(values, gain)
+        return (normed * cos + pltpu.roll(normed, dim // 2, 1) * sin).astype(BF16).astype(F32)
+
+    small[0].wait()
+    small[1].wait()
+    key = jnp.dot(hn[...], wk[...], preferred_element_type=F32)
+    val = jnp.dot(hn[...], wv[...], preferred_element_type=F32).astype(BF16).astype(F32)
+    for g in range(kv_heads):
+        cols = slice(g * dim, (g + 1) * dim)
+        turned_k = turned(key[:, cols], kn_ref[...].astype(F32))
+        for r in range(8 // kv_heads):
+            rows = pl.ds(g + kv_heads * r, b_dev, stride=8)
+            knew[rows, :] = turned_k
+            vnew[rows, :] = val[:, cols]
+    for i in range(n_q):
+        copy_q(i).wait()
+        part = jnp.dot(hn[...], wq[:, i * qc:(i + 1) * qc], preferred_element_type=F32)
+        for j in range(qc // dim):
+            qs[pl.ds(i * (qc // dim) + j, b_dev, stride=q_heads), :] = turned(
+                part[:, j * dim:(j + 1) * dim], qn_ref[...].astype(F32))
+
+    row_slot = lax.broadcasted_iota(jnp.int32, (lanes, dim), 0) // kv_heads
+    lane = lax.broadcasted_iota(jnp.int32, (q_heads, lanes), 1)
+    own_head = lax.rem(lane, kv_heads) == lax.broadcasted_iota(jnp.int32, (q_heads, lanes), 0) // rep
+    lane_slot = jnp.where(own_head, lane // kv_heads, lanes)
+
+    @pl.loop(0, n_blk)
+    def _(b):
+        for c in copy_in(b):
+            c.wait()
+        scores = []
+        for j in range(blk):
+            t = b * blk + j
+            size = len_ref[t]
+            here = row_slot == size
+            fresh = pl.ds(pl.multiple_of(t * 8, 8), 8)
+            k_row = jnp.concatenate([knew[fresh, :]] * (lanes // 8), axis=0)
+            v_row = jnp.concatenate([vnew[fresh, :]] * (lanes // 8), axis=0)
+            k_tok = jnp.where(here, k_row, kbuf[t].astype(F32)).astype(BF16)
+            kbuf[t] = k_tok
+            vbuf[t] = jnp.where(here, v_row, vbuf[t].astype(F32)).astype(BF16)
+            q_tok = qs[pl.ds(pl.multiple_of(t * q_heads, q_heads), q_heads), :].astype(BF16)
+            score = lax.dot_general(q_tok, k_tok, (((1,), (1,)), ((), ())), preferred_element_type=F32)
+            scores.append(jnp.where(lane_slot <= size, score * dim ** -0.5, -1e30))
+        score = jnp.concatenate(scores, axis=0)
+        weight = jnp.exp(score - jnp.max(score, axis=1, keepdims=True))
+        prob = (weight / jnp.sum(weight, axis=1, keepdims=True)).astype(BF16)
+        for j in range(blk):
+            t = b * blk + j
+            os[pl.ds(pl.multiple_of(t * q_heads, q_heads), q_heads), :] = jnp.dot(
+                prob[j * q_heads:(j + 1) * q_heads, :], vbuf[t], preferred_element_type=F32)
+        for c in copy_out(b):
+            c.start()
+
+    for h in range(q_heads):
+        att[:, h * dim:(h + 1) * dim] = os[pl.ds(h, b_dev, stride=q_heads), :].astype(BF16)
+    for i in range(n_o):
+        copy_o(i).wait()
+        cols = slice(i * oc, (i + 1) * oc)
+        out = jnp.dot(att[...], wo[:, cols], preferred_element_type=F32)
+        xmid_ref[:, cols] = (x_ref[:, cols].astype(F32) + out).astype(BF16)
+    h_moe = rms(xmid_ref[...].astype(F32), lnm_ref[...].astype(F32)).astype(BF16)
+    h_ref[...] = h_moe
+    small[2].wait()
+    logits = jnp.transpose(jnp.dot(h_moe, wr[...], preferred_element_type=F32))
+    experts = logits.shape[0]
+    e_local = experts // ep_size
+    expert = lax.broadcasted_iota(jnp.int32, (experts, b_dev), 0)
+    chosen = expert == idx_ref[0:1, :]
+    for k in range(1, idx_ref.shape[0]):
+        chosen = chosen | (expert == idx_ref[k:k + 1, :])
+    top = jnp.max(jnp.where(chosen, logits, -1e30), axis=0, keepdims=True)
+    mass = jnp.where(chosen, jnp.exp(logits - top), 0.0)
+    mass = mass / jnp.sum(mass, axis=0, keepdims=True)
+    local = jnp.where(chosen, lax.rem(expert, e_local), 0).astype(F32)
+    meta_ref[0:ep_size, :] = jnp.sum(local.reshape(ep_size, e_local, b_dev), axis=1)
+    meta_ref[ep_size:2 * ep_size, :] = jnp.sum(mass.reshape(ep_size, e_local, b_dev), axis=1)
+
+    for b in range(n_blk):
+        for c in copy_out(b):
+            c.wait()
+
+
+def attend_block(ep_size, x_in, k_cache, v_cache, cache_len, topk_idx, ln_attn, w_q, w_k, w_v, q_norm, k_norm, w_o, ln_moe, w_router):
+    b_dev, hidden = x_in.shape
+    _, n_slots, kv_heads, dim = k_cache.shape
+    q_width, kv_width, experts = w_q.shape[1], w_k.shape[1], w_router.shape[1]
+    q_heads = q_width // dim
+    lanes = n_slots * kv_heads
+    freq = ROPE_BASE ** (-jnp.arange(dim // 2, dtype=F32) * 2.0 / dim)
+    angles = cache_len.astype(F32)[:, None] * freq
+    cosine, sine = jnp.cos(angles), jnp.sin(angles)
+    cos = jnp.concatenate([cosine, cosine], axis=1)
+    sin = jnp.concatenate([-sine, sine], axis=1)
+    n_q, n_o, n_blk = 8, 4, 8
+    vmem, dma, far = pltpu.VMEM, pltpu.SemaphoreType.DMA, pl.BlockSpec(memory_space=pl.ANY)
+    near = pl.BlockSpec(memory_space=pltpu.VMEM)
+    flat = (b_dev, lanes, dim)
+    x_mid, h_moe, meta, k_new, v_new = pl.pallas_call(
+        functools.partial(attend_kernel, ep_size),
+        out_shape=(jax.ShapeDtypeStruct((b_dev, hidden), BF16), jax.ShapeDtypeStruct((b_dev, hidden), BF16),
+                   jax.ShapeDtypeStruct((2 * ep_size, b_dev), F32),
+                   jax.ShapeDtypeStruct(flat, BF16), jax.ShapeDtypeStruct(flat, BF16)),
+        in_specs=[pl.BlockSpec(memory_space=pltpu.SMEM)] + [near] * 8 + [far] * 7,
+        out_specs=(near, near, near, far, far),
+        scratch_shapes=[
+            vmem((hidden, q_width), BF16), vmem((hidden, kv_width), BF16), vmem((hidden, kv_width), BF16),
+            vmem((q_width, hidden), BF16), vmem((hidden, experts), BF16), vmem(flat, BF16), vmem(flat, BF16),
+            vmem((b_dev * q_heads, dim), F32), vmem((b_dev * q_heads, dim), F32),
+            vmem((b_dev * 8, dim), F32), vmem((b_dev * 8, dim), F32),
+            vmem((b_dev, hidden), BF16), vmem((b_dev, q_width), BF16),
+            dma((n_q,)), dma((3,)), dma((n_o,)), dma((2, n_blk)), dma((2, n_blk)),
+        ],
+        compiler_params=pltpu.CompilerParams(vmem_limit_bytes=67043328),
+        name='attend',
+    )(cache_len, x_in, cos, sin, topk_idx.T, ln_attn[None], q_norm[None], k_norm[None], ln_moe[None],
+      w_q, w_k, w_v, w_o, w_router, k_cache.reshape(flat), v_cache.reshape(flat))
+    return x_mid, h_moe, meta, k_new.reshape(k_cache.shape), v_new.reshape(v_cache.shape)
 
 
 def moe_kernel(ep_size, h_ref, x_ref, meta_ref, wg_hbm, wu_hbm, wd_hbm, out_ref, flag_ref,
@@ -341,27 +471,22 @@
     )(h_moe, x_mid, meta, w_gate, w_up, w_down)
 
 
-def moe_general(ep_size, h_moe, x_mid, topk_idx, gate_wts, w_gate, w_up, w_down):
+def moe_general(ep_size, h_moe, x_mid, meta, w_gate, w_up, w_down):
     b_dev, hidden = h_moe.shape
-    e_local = w_gate.shape[0]
-    owner = topk_idx // e_local
-    hot = owner[:, None, :] == jnp.arange(ep_size)[None, :, None]
-    local = jnp.sum(jnp.where(hot, (topk_idx % e_local)[:, None, :], 0), axis=2).T
-    wts = jnp.sum(jnp.where(hot, gate_wts[:, None, :], 0.0), axis=2)
     rows = lax.all_to_all(jnp.broadcast_to(h_moe[None], (ep_size, b_dev, hidden)), 'ep', 0, 0, tiled=True)
     rows = rows.reshape(ep_size * b_dev, hidden)
-    ids = lax.all_to_all(local[:, None, :], 'ep', 0, 0, tiled=True).reshape(ep_size * b_dev)
+    ids = lax.all_to_all(meta[:ep_size, None, :], 'ep', 0, 0, tiled=True).reshape(ep_size * b_dev)
 
     def one(e, done):
         gate = jnp.dot(rows, w_gate[e], preferred_element_type=F32)
         up = jnp.dot(rows, w_up[e], preferred_element_type=F32)
         act = (jax.nn.silu(gate) * up).astype(BF16)
         y = jnp.dot(act, w_down[e], preferred_element_type=F32).astype(BF16)
-        return jnp.where((ids == e)[:, None], y, done)
-
-    y = lax.fori_loop(0, e_local, one, jnp.zeros(rows.shape, BF16))
+        return jnp.where((ids == e.astype(F32))[:, None], y, done)
+
+    y = lax.fori_loop(0, w_gate.shape[0], one, jnp.zeros(rows.shape, BF16))
     back = lax.all_to_all(y.reshape(ep_size, b_dev, hidden), 'ep', 0, 0, tiled=True)
-    total = jnp.sum(back.astype(F32) * wts.T[:, :, None], axis=0)
+    total = jnp.sum(back.astype(F32) * meta[ep_size:, :, None], axis=0)
     return (x_mid.astype(F32) + total).astype(BF16)
 
 
@@ -374,17 +499,11 @@
     out_specs = (row_spec, row_spec, row_spec)
 
     def device_step(x_in, k_cache, v_cache, cache_len, topk_idx, ln_attn, w_q, w_k, w_v, q_norm, k_norm, w_o, ln_moe, w_router, w_gate, w_up, w_down):
-        x_mid, k_full, v_full = attend_block(x_in, k_cache, v_cache, cache_len, ln_attn, w_q, w_k, w_v, q_norm, k_norm, w_o)
-        h_moe, gate_wts = route_gate(x_mid, ln_moe, w_router, topk_idx)
-        e_local = w_gate.shape[0]
-        owner = topk_idx // e_local
-        hot = owner[:, None, :] == jnp.arange(ep_size)[None, :, None]
-        local = jnp.sum(jnp.where(hot, (topk_idx % e_local)[:, None, :], 0), axis=2).astype(F32)
-        wts = jnp.sum(jnp.where(hot, gate_wts[:, None, :], 0.0), axis=2)
-        meta = jnp.concatenate([local, wts], axis=1).T
+        x_mid, h_moe, meta, k_full, v_full = attend_block(
+            ep_size, x_in, k_cache, v_cache, cache_len, topk_idx, ln_attn, w_q, w_k, w_v, q_norm, k_norm, w_o, ln_moe, w_router)
         fast, most = moe_block(ep_size, h_moe, x_mid, meta, w_gate, w_up, w_down)
         x_out = lax.cond(most[0, 0] > SEATS,
-                         lambda: moe_general(ep_size, h_moe, x_mid, topk_idx, gate_wts, w_gate, w_up, w_down),
+                         lambda: moe_general(ep_size, h_moe, x_mid, meta, w_gate, w_up, w_down),
                          lambda: fast)
         return x_out, k_full, v_full
 

time: 163 us -> 145 us (0.89)
  Pallas kernels: 105 us -> 136 us
  matrix products: 26 us -> 0 us
  other arithmetic: 14.8 us -> 1.74 us
  local copies, waits for them, and re-layouts: 15.2 us -> 5.71 us
    pallas_call x0 -> x1, Pallas kernels: none -> 31.1 us  [attend_block(): pl.pallas_call(functools.partial(attend_kernel, ep_size), out_shape=(jax....]
    dot_general x6 -> x0, matrix products: 19.9 us -> none  [the longest x1 8.56 us: attend_block(): jnp.dot(attn_out, w_o, preferred_element_type=jnp.float32)]
    select_n x2 -> x0, other arithmetic: 8.09 us -> none  [the longest x1 8.08 us: attend_block(): k_full = jnp.where(is_new, k_new[:, None], k_cache)]
    gather x5 -> x0, local copies, waits for them, and re-layouts: 7.12 us -> none  [route_gate(): jnp.take_along_axis(logits, topk_idx, axis=1)]
    sub x1 -> x0, matrix products: 6.17 us -> none  [attend_block(): jax.nn.softmax(jnp.where(seen, scores, -1e+30), axis=-1)]
    unnamed x24 -> x1, local copies, waits for them, and re-layouts: 6.7 us -> 1.88 us
    broadcast_in_dim x1 -> x2, local copies, waits for them, and re-layouts: 0.04 us -> 2.58 us  [the longest x1 1.3 us: attend_block(): ln_moe[None]]
    reduce_sum x6 -> x0, other arithmetic: 2.17 us -> none  [the longest x3 2.12 us: norm_scale(): jnp.mean(values * values, axis=-1, keepdims=True) + NORM_EPS]
where the time goes in v2:
time: 145 us
  Pallas kernels  136 us (94%)
  local copies, waits for them, and re-layouts  5.71 us (4%)
  other arithmetic  1.74 us (1%)
    pallas_call x1, Pallas kernels, moe_block(): pl.pallas_call(functools.partial(moe_kernel, ep_size), out_shape=(jax.Sha...  105 us
    pallas_call x1, Pallas kernels, attend_block(): pl.pallas_call(functools.partial(attend_kernel, ep_size), out_shape=(jax....  31.1 us

profile of v2, /device:TPU:113, one launch (start us, length us, event | category | flops | bytes accessed | tf_op | source)
XLA Modules:
  0.0 144.5 jit_solution(6250629653363274346)
XLA Ops:
  0.6 0.7 convert_element_type.39
  1.3 0.3 fusion.20
  1.6 0.8 pad_maximum_fusion
  2.4 1.3 broadcast_in_dim.45.lna_ref
  3.7 1.3 broadcast_in_dim.48.lnm_ref
  5.0 31.1 %attend.1 = (bf16[128,2048]{1,0:T(8,128)(2,1)}, bf16[128,2048]{1,0:T(8,128)(2,1)}, f32[16,128]{1,0:T(8,128)}, bf16[128,128,128]{2,1,0:T(8,128)(2,1)}, bf16[128,128,128]{2,1,0:T(8,128)(2,1)}) custom-call(s32[128]{0:T(128)} %len_ref.1, bf16[128,2048]{1,0:T(8,128)(2,1)} %x_ref.1, f32[128,128]{1,0:T(8,128)} %get-tuple-element.206.cos_ref, ...), custom_call_target="tpu_custom_call" | custom-call | tf_op jit(solution)/shard_map/attend/pallas_call | solution.py:172
  36.0 104.7 %moe.1 = (bf16[128,2048]{1,0:T(8,128)(2,1)}, f32[8,128]{1,0:T(8,128)}) custom-call(bf16[128,2048]{1,0:T(8,128)(2,1)} %get-tuple-element.156.h_ref, bf16[128,2048]{1,0:T(8,128)(2,1)} %get-tuple-element.157.x_ref, f32[16,128]{1,0:T(8,128)} %get-tuple-element.158.meta_ref, bf16[16,2048,768]{2,1,0:T(8,128)(2,1)} %wg_hbm.1, bf16[16,2048,768]{2,1,0:T(8,128)(2,1)} %wu_hbm.1, ...), custom_call_target="tpu_custom_call" | custom-call | tf_op jit(solution)/shard_map/moe/pallas_call | solution.py:451
  140.7 1.2 slice.9
  142.6 1.9 %copy.29 = bf16[128,2048]{1,0:T(8,128)(2,1)} copy(bf16[128,2048]{1,0:T(8,128)(2,1)} %get-tuple-element.284) | data formatting | bytes 1048576
  (2 shorter events, 0.0 us)

commit v3 on v2

v3 whole, which is shorter than its diff:
```python
import functools
import math

import jax
import jax.numpy as jnp
from jax import lax
from jax.experimental import pallas as pl
from jax.experimental.pallas import tpu as pltpu
from jax.sharding import PartitionSpec as P

ROPE_BASE = 1000000.0
NORM_EPS = 1e-6
MESH = pl.DeviceIdType.MESH
F32 = jnp.float32
BF16 = jnp.bfloat16
SEATS = 128
SPLIT = 4
DEEP = 2


def rms(values):
    return values * lax.rsqrt(jnp.mean(values * values, axis=-1, keepdims=True) + NORM_EPS)


def rms_rows(values, gain_ref, out_ref):
    normed = rms(values)
    lanes = gain_ref.shape[1]
    for i in range(gain_ref.shape[0]):
        cols = slice(i * lanes, (i + 1) * lanes)
        out_ref[:, cols] = (normed[:, cols] * gain_ref[i:i + 1, :].astype(F32)).astype(BF16)


def attend_kernel(ep_size, len_ref, x_ref, row_ref, idx_ref, lna_ref, qn_ref, kn_ref, lnm_ref,
                  wq_hbm, wk_hbm, wv_hbm, wo_hbm, wr_hbm, kc_hbm, vc_hbm,
                  xmid_ref, h_ref, meta_ref, ko_hbm, vo_hbm,
                  wq, wk, wv, wo, wr, kbuf, vbuf, qs, os, knew, vnew, hn, att, part,
                  s_q, s_kv, s_o, s_c, s_out):
    b_dev, hidden = x_ref.shape
    _, lanes, dim = kbuf.shape
    q_width = wq.shape[1]
    q_heads, kv_heads = q_width // dim, wk.shape[1] // dim
    n_q, n_o = s_q.shape[0], s_o.shape[0]
    n_blk = s_c.shape[1]
    blk = b_dev // n_blk
    qc, oc = q_width // n_q, hidden // n_o
    rep = q_heads // kv_heads

    def copy_q(i):
        cols = pl.ds(pl.multiple_of(i * qc, qc), qc)
        return pltpu.make_async_copy(wq_hbm.at[:, cols], wq.at[:, cols], s_q.at[i])

    def copy_o(i):
        cols = pl.ds(pl.multiple_of(i * oc, oc), oc)
        return pltpu.make_async_copy(wo_hbm.at[:, cols], wo.at[:, cols], s_o.at[i])

    def copy_in(b):
        rows = pl.ds(b * blk, blk)
        return (pltpu.make_async_copy(kc_hbm.at[rows], kbuf.at[rows], s_c.at[0, b]),
                pltpu.make_async_copy(vc_hbm.at[rows], vbuf.at[rows], s_c.at[1, b]))

    def copy_out(b):
        rows = pl.ds(b * blk, blk)
        return (pltpu.make_async_copy(kbuf.at[rows], ko_hbm.at[rows], s_out.at[0, b]),
                pltpu.make_async_copy(vbuf.at[rows], vo_hbm.at[rows], s_out.at[1, b]))

    small = (pltpu.make_async_copy(wk_hbm, wk, s_kv.at[0]), pltpu.make_async_copy(wv_hbm, wv, s_kv.at[1]),
             pltpu.make_async_copy(wr_hbm, wr, s_kv.at[2]))
    for c in small[:2]:
        c.start()
    for i in range(n_q):
        copy_q(i).start()

    x = x_ref[...].astype(F32)
    rms_rows(x, lna_ref, hn)
    pair = lax.rem(lax.broadcasted_iota(jnp.int32, (b_dev, dim), 1), dim // 2).astype(F32)
    freq = jnp.exp(pair * (-2.0 / dim * math.log(ROPE_BASE)))
    angle = jnp.transpose(jnp.broadcast_to(row_ref[...].astype(F32), (dim, b_dev))) * freq
    cos = jnp.cos(angle)
    sin = jnp.where(lax.broadcasted_iota(jnp.int32, (b_dev, dim), 1) < dim // 2, -1.0, 1.0) * jnp.sin(angle)

    def turned(values, gain):
        normed = rms(values) * gain
        return (normed * cos + pltpu.roll(normed, dim // 2, 1) * sin).astype(BF16).astype(F32)

    small[0].wait()
    small[1].wait()
    key = jnp.dot(hn[...], wk[...], preferred_element_type=F32)
    val = jnp.dot(hn[...], wv[...], preferred_element_type=F32).astype(BF16).astype(F32)
    for g in range(kv_heads):
        cols = slice(g * dim, (g + 1) * dim)
        turned_k = turned(key[:, cols], kn_ref[...].astype(F32))
        for r in range(8 // kv_heads):
            rows = pl.ds(g + kv_heads * r, b_dev, stride=8)
            knew[rows, :] = turned_k
            vnew[rows, :] = val[:, cols]
    def spread(i):
        for j in range(qc // dim):
            qs[pl.ds(i * (qc // dim) + j, b_dev, stride=q_heads), :] = turned(
                part[i % 2, :, j * dim:(j + 1) * dim], qn_ref[...].astype(F32))

    for i in range(n_q):
        copy_q(i).wait()
        if i == 1:
            for b in range(n_blk):
                for c in copy_in(b):
                    c.start()
        if i == 4:
            for j in range(n_o):
                copy_o(j).start()
            small[2].start()
        part[i % 2] = jnp.dot(hn[...], wq[:, i * qc:(i + 1) * qc], preferred_element_type=F32)
        if i:
            spread(i - 1)
    spread(n_q - 1)

    row_slot = lax.broadcasted_iota(jnp.int32, (lanes, dim), 0) // kv_heads
    lane = lax.broadcasted_iota(jnp.int32, (q_heads, lanes), 1)
    own_head = lax.rem(lane, kv_heads) == lax.broadcasted_iota(jnp.int32, (q_heads, lanes), 0) // rep
    lane_slot = jnp.where(own_head, lane // kv_heads, lanes)

    @pl.loop(0, n_blk)
    def _(b):
        for c in copy_in(b):
            c.wait()
        scores = []
        for j in range(blk):
            t = b * blk + j
            size = len_ref[t]
            here = row_slot == size
            fresh = pl.ds(pl.multiple_of(t * 8, 8), 8)
            k_row = jnp.concatenate([knew[fresh, :]] * (lanes // 8), axis=0)
            v_row = jnp.concatenate([vnew[fresh, :]] * (lanes // 8), axis=0)
            k_tok = jnp.where(here, k_row, kbuf[t].astype(F32)).astype(BF16)
            kbuf[t] = k_tok
            vbuf[t] = jnp.where(here, v_row, vbuf[t].astype(F32)).astype(BF16)
            q_tok = qs[pl.ds(pl.multiple_of(t * q_heads, q_heads), q_heads), :].astype(BF16)
            score = lax.dot_general(q_tok, k_tok, (((1,), (1,)), ((), ())), preferred_element_type=F32)
            scores.append(jnp.where(lane_slot <= size, score * dim ** -0.5, -1e30))
        score = jnp.concatenate(scores, axis=0)
        weight = jnp.exp(score - jnp.max(score, axis=1, keepdims=True))
        prob = (weight / jnp.sum(weight, axis=1, keepdims=True)).astype(BF16)
        for j in range(blk):
            t = b * blk + j
            os[pl.ds(pl.multiple_of(t * q_heads, q_heads), q_heads), :] = jnp.dot(
                prob[j * q_heads:(j + 1) * q_heads, :], vbuf[t], preferred_element_type=F32)
        for c in copy_out(b):
            c.start()

    for h in range(q_heads):
        att[:, h * dim:(h + 1) * dim] = os[pl.ds(h, b_dev, stride=q_heads), :].astype(BF16)
    for i in range(n_o):
        copy_o(i).wait()
        cols = slice(i * oc, (i + 1) * oc)
        out = jnp.dot(att[...], wo[:, cols], preferred_element_type=F32)
        xmid_ref[:, cols] = (x_ref[:, cols].astype(F32) + out).astype(BF16)
    rms_rows(xmid_ref[...].astype(F32), lnm_ref, h_ref)
    small[2].wait()
    logits = jnp.transpose(jnp.dot(h_ref[...], wr[...], preferred_element_type=F32))
    experts = logits.shape[0]
    e_local = experts // ep_size
    expert = lax.broadcasted_iota(jnp.int32, (experts, b_dev), 0)
    chosen = expert == idx_ref[0:1, :]
    for k in range(1, idx_ref.shape[0]):
        chosen = chosen | (expert == idx_ref[k:k + 1, :])
    top = jnp.max(jnp.where(chosen, logits, -1e30), axis=0, keepdims=True)
    mass = jnp.where(chosen, jnp.exp(logits - top), 0.0)
    mass = mass / jnp.sum(mass, axis=0, keepdims=True)
    local = jnp.where(chosen, lax.rem(expert, e_local), 0).astype(F32)
    meta_ref[0:ep_size, :] = jnp.sum(local.reshape(ep_size, e_local, b_dev), axis=1)
    meta_ref[ep_size:2 * ep_size, :] = jnp.sum(mass.reshape(ep_size, e_local, b_dev), axis=1)

    for b in range(n_blk):
        for c in copy_out(b):
            c.wait()


def attend_block(ep_size, x_in, k_cache, v_cache, cache_len, topk_idx, ln_attn, w_q, w_k, w_v, q_norm, k_norm, w_o, ln_moe, w_router):
    b_dev, hidden = x_in.shape
    _, n_slots, kv_heads, dim = k_cache.shape
    q_width, kv_width, experts = w_q.shape[1], w_k.shape[1], w_router.shape[1]
    q_heads = q_width // dim
    lanes = n_slots * kv_heads
    n_q, n_o, n_blk = 8, 4, 8
    vmem, dma, far = pltpu.VMEM, pltpu.SemaphoreType.DMA, pl.BlockSpec(memory_space=pl.ANY)
    near = pl.BlockSpec(memory_space=pltpu.VMEM)
    flat = (b_dev, lanes, dim)
    x_mid, h_moe, meta, k_new, v_new = pl.pallas_call(
        functools.partial(attend_kernel, ep_size),
        out_shape=(jax.ShapeDtypeStruct((b_dev, hidden), BF16), jax.ShapeDtypeStruct((b_dev, hidden), BF16),
                   jax.ShapeDtypeStruct((2 * ep_size, b_dev), F32),
                   jax.ShapeDtypeStruct(flat, BF16), jax.ShapeDtypeStruct(flat, BF16)),
        in_specs=[pl.BlockSpec(memory_space=pltpu.SMEM)] + [near] * 7 + [far] * 7,
        out_specs=(near, near, near, far, far),
        scratch_shapes=[
            vmem((hidden, q_width), BF16), vmem((hidden, kv_width), BF16), vmem((hidden, kv_width), BF16),
            vmem((q_width, hidden), BF16), vmem((hidden, experts), BF16), vmem(flat, BF16), vmem(flat, BF16),
            vmem((b_dev * q_heads, dim), F32), vmem((b_dev * q_heads, dim), F32),
            vmem((b_dev * 8, dim), F32), vmem((b_dev * 8, dim), F32),
            vmem((b_dev, hidden), BF16), vmem((b_dev, q_width), BF16), vmem((2, b_dev, q_width // n_q), F32),
            dma((n_q,)), dma((3,)), dma((n_o,)), dma((2, n_blk)), dma((2, n_blk)),
        ],
        compiler_params=pltpu.CompilerParams(vmem_limit_bytes=67043328),
        name='attend',
    )(cache_len, x_in, cache_len[None], topk_idx.T, ln_attn.reshape(-1, dim), q_norm[None], k_norm[None], ln_moe.reshape(-1, dim),
      w_q, w_k, w_v, w_o, w_router, k_cache.reshape(flat), v_cache.reshape(flat))
    return x_mid, h_moe, meta, k_new.reshape(k_cache.shape), v_new.reshape(v_cache.shape)


def moe_kernel(ep_size, h_ref, x_ref, meta_ref, wg_hbm, wu_hbm, wd_hbm, out_ref, flag_ref,
               xall, mall, perm, keys, share, xg_even, xg_odd, hid, ys, ybuf, yrecv, acc, recv1, recv2, fin,
               wg, wu, wd, s_w, s_d, s_own, s_fwd, r_x, s_meta, r_meta,
               s_y, r_y, s_1, r_1, s_2, r_2, s_f, r_f):
    b_dev, hidden = h_ref.shape
    e_local, _, ff = wg_hbm.shape
    n_chip = ep_size // 2
    half = b_dev // 2
    depth = hidden // DEEP
    wide = hidden // SPLIT
    side = wide // 2
    n_a, n_b = wg.shape[0], wd.shape[0]
    per = wd.shape[1]
    groups = e_local // per
    me = lax.axis_index('ep')
    chip, core = me // 2, me % 2
    right = lax.rem(chip + 1, n_chip)
    left = lax.rem(chip + n_chip - 1, n_chip)
    far = lax.rem(chip + 2, n_chip)
    dev_r, dev_l, mate = right * 2 + core, left * 2 + core, chip * 2 + 1 - core

    def load_a(i):
        slot = lax.rem(i, n_a)
        rows = pl.ds(pl.multiple_of(i // e_local * depth, depth), depth)
        e = lax.rem(i, e_local)
        return (pltpu.make_async_copy(wg_hbm.at[e, rows], wg.at[slot], s_w.at[0, slot]),
                pltpu.make_async_copy(wu_hbm.at[e, rows], wu.at[slot], s_w.at[1, slot]))

    def load_b(i):
        slot = lax.rem(i, n_b)
        q, g = i // groups, lax.rem(i, groups)
        cols = pl.ds(pl.multiple_of(q * wide, wide), wide)
        return pltpu.make_async_copy(wd_hbm.at[pl.ds(g * per, per), :, cols], wd.at[slot], s_d.at[slot])

    for e in range(n_a):
        for c in load_a(e):
            c.start()
    for i in range(n_b):
        load_b(i).start()

    barrier = pltpu.get_barrier_semaphore()
    for k in range(1, ep_size):
        pl.semaphore_signal(barrier, inc=1, device_id={'ep': lax.rem(me + k, ep_size)}, device_id_type=MESH)
    pl.semaphore_wait(barrier, ep_size - 1)

    def part(h):
        return pl.ds(h * half, half)

    def send_own(k, h, target, sem):
        cols = pl.ds(k * depth, depth)
        return pltpu.make_async_remote_copy(h_ref.at[part(h), cols], xall.at[k, me, part(h)], s_own.at[k, sem],
                                            r_x.at[k, me, h], device_id={'ep': target}, device_id_type=MESH)

    def forward(k, src, h, target, sem):
        return pltpu.make_async_remote_copy(xall.at[k, src, part(h)], xall.at[k, src, part(h)], s_fwd.at[k, sem],
                                            r_x.at[k, src, h], device_id={'ep': target}, device_id_type=MESH)

    def send_meta(k):
        return pltpu.make_async_remote_copy(meta_ref, mall.at[me], s_meta.at[k - 1], r_meta.at[me],
                                            device_id={'ep': lax.rem(me + k, ep_size)}, device_id_type=MESH)

    dev_f = far * 2 + core
    outgoing = ((0, dev_r), (1, dev_l), (1, dev_r), (0, dev_l), (0, mate), (1, mate))
    passed = ((dev_l, 0, dev_r), (dev_r, 1, dev_l), (dev_l, 0, mate), (dev_r, 1, mate))
    handed = ((dev_l, 1, mate), (dev_r, 0, mate), (dev_f, 0, mate), (dev_f, 1, mate))

    def own(k):
        for i, (h, target) in enumerate(outgoing):
            send_own(k, h, target, i).start()

    def pump(k):
        for i, (src, h, target) in enumerate(passed):
            if target is not mate:
                forward(k, src, h, target, i).wait_recv()
        for i, (src, h, target) in enumerate(passed):
            forward(k, src, h, target, i).start()

    def hand(k):
        for i, (src, h, target) in enumerate(handed):
            forward(k, src, h, target, 4 + i).wait_recv()
            forward(k, src, h, target, 4 + i).start()

    def arrive(k):
        for c in range(n_chip):
            src = lax.rem(chip + c, n_chip) * 2 + 1 - core
            for h in range(2):
                forward(k, src, h, mate, 0).wait_recv()

    for k in range(1, ep_size):
        send_meta(k).start()
    own(0)
    for k in range(DEEP):
        xall[k, me] = h_ref[:, k * depth:(k + 1) * depth]
    mall[me] = meta_ref[...]
    pump(0)
    own(1)

    for k in range(1, ep_size):
        src = lax.rem(me + k, ep_size)
        pltpu.make_async_remote_copy(meta_ref, mall.at[src], s_meta.at[k - 1], r_meta.at[src],
                                     device_id={'ep': src}, device_id_type=MESH).wait_recv()
    lower = lax.broadcasted_iota(jnp.int32, (b_dev, b_dev), 0) < lax.broadcasted_iota(jnp.int32, (b_dev, b_dev), 1)
    before = jnp.where(lower, 1.0, 0.0).astype(BF16)
    ids16 = lax.broadcasted_iota(jnp.int32, (e_local, b_dev), 0).astype(F32)
    keys[...] = jnp.zeros_like(keys)
    counts = jnp.zeros((e_local, 1), F32)
    for src in range(ep_size):
        row = mall[src, pl.ds(me, 1), :]
        hot = jnp.where(ids16 == row, 1.0, 0.0)
        ranks = jnp.dot(hot.astype(BF16), before, preferred_element_type=F32) + counts
        rank = jnp.sum(hot * ranks, axis=0, keepdims=True)
        keys[pl.ds(src, 1), :] = row * SEATS + rank
        keys[pl.ds(ep_size + src, 1), :] = mall[src, pl.ds(ep_size + me, 1), :]
        keys[pl.ds(2 * ep_size + src, 1), :] = mall[src, pl.ds(ep_size + mate, 1), :]
        counts = counts + jnp.sum(hot, axis=1, keepdims=True)
    keyt = jnp.transpose(keys[...])
    for b in range(2 * ep_size):
        share[b] = jnp.broadcast_to(keyt[:, ep_size + b:ep_size + b + 1], (b_dev, b_dev))
    most = jnp.zeros((e_local, 1), F32)
    for dev in range(ep_size):
        total = jnp.zeros((e_local, 1), F32)
        for src in range(ep_size):
            hot = jnp.where(ids16 == mall[src, pl.ds(dev, 1), :], 1.0, 0.0)
            total = total + jnp.sum(hot, axis=1, keepdims=True)
        most = jnp.maximum(most, total)
    flag_ref[0] = jnp.max(most)

    seat_cols = lax.broadcasted_iota(jnp.int32, (b_dev, 4 * SEATS), 1).astype(F32)
    for b in range(ep_size):
        col = jnp.transpose(keys[...])[:, b:b + 1]

        @pl.loop(0, e_local // 4)
        def _(j):
            base = (j * (4 * SEATS)).astype(F32)
            hot = jnp.where(seat_cols + base == col, 1.0, 0.0).astype(BF16)
            perm[b * b_dev:(b + 1) * b_dev, pl.ds(pl.multiple_of(j * (4 * SEATS), 4 * SEATS), 4 * SEATS)] = hot

    hand(0)
    arrive(0)

    seat_rows = lax.broadcasted_iota(jnp.int32, (SEATS, b_dev), 0).astype(F32)

    n_ff = ff // side

    def pick_rows(k, e, out):
        base = (e * SEATS).astype(F32)
        pick = jnp.concatenate(
            [jnp.where(keys[b:b + 1, :] == seat_rows + base, 1.0, 0.0).astype(BF16) for b in range(ep_size)], axis=1)
        for n in range(depth // 512):
            cols = slice(n * 512, (n + 1) * 512)
            rows = xall[k, :, :, cols].reshape(ep_size * b_dev, 512)
            out[:, cols] = jnp.dot(pick, rows, preferred_element_type=F32).astype(BF16)

    def project(k, e, rows):
        slot = lax.rem(k * e_local + e, n_a)
        for n in range(n_ff):
            cols = slice(n * side, (n + 1) * side)
            gate = jnp.dot(rows[...], wg[slot, :, cols], preferred_element_type=F32)
            up = jnp.dot(rows[...], wu[slot, :, cols], preferred_element_type=F32)
            at = e * (2 * n_ff) + 2 * n
            if k:
                gate = gate + acc[at]
                up = up + acc[at + 1]
            if k < DEEP - 1:
                acc[at] = gate
                acc[at + 1] = up
            else:
                hid[e, :, cols] = (gate * jax.nn.sigmoid(gate) * up).astype(BF16)

    def refill(item):
        @pl.when(item + n_a < DEEP * e_local)
        def _():
            for c in load_a(item + n_a):
                c.start()

    def down(q, g):
        i = q * groups + g
        slot = lax.rem(i, n_b)
        load_b(i).wait()
        for j in range(per):
            e = g * per + j
            ys[pl.ds(pl.multiple_of(e * SEATS, SEATS), SEATS), :] = jnp.dot(
                hid[e], wd[slot, j], preferred_element_type=F32).astype(BF16)

        @pl.when(i + n_b < SPLIT * groups)
        def _():
            load_b(i + n_b).start()

    for k in range(DEEP):
        pick_rows(k, jnp.int32(0), xg_even)

        @pl.loop(0, e_local // 2)
        def _(p):
            for odd, (now, later) in enumerate(((xg_even, xg_odd), (xg_odd, xg_even))):
                e = 2 * p + odd
                for c in load_a(k * e_local + e):
                    c.wait()
                pick_rows(k, jnp.minimum(e + 1, e_local - 1), later)
                project(k, e, now)
                refill(k * e_local + e)
            if k + 1 < DEEP:
                @pl.when(p == 0)
                def _():
                    pump(k + 1)
                    if k + 2 < DEEP:
                        own(k + 2)

                @pl.when(p == 3)
                def _():
                    hand(k + 1)
            else:
                @pl.when(lax.rem(p, per // 2) == per // 2 - 1)
                def _():
                    down(0, p // (per // 2))

        if k + 1 < DEEP:
            arrive(k + 1)

    def chip_of(m):
        return lax.rem(chip + 2 + m, n_chip)

    def send_y(q, m):
        blocks = pl.ds(2 * chip_of(m), 2)
        return pltpu.make_async_remote_copy(ybuf.at[lax.rem(q, 2), 1 - core, blocks], yrecv.at[q, blocks],
                                            s_y.at[q, m], r_y.at[q, m], device_id={'ep': mate}, device_id_type=MESH)

    def send_1(q, d):
        block = far * 2 + d
        return pltpu.make_async_remote_copy(acc.at[q * ep_size + block], recv1.at[d, q], s_1.at[d, q], r_1.at[d, q],
                                            device_id={'ep': dev_l if d else dev_r}, device_id_type=MESH)

    def send_2(q, d):
        block = (left if d else right) * 2
        return pltpu.make_async_remote_copy(acc.at[pl.ds(q * ep_size + block, 2)], recv2.at[d, q], s_2.at[d, q], r_2.at[d, q],
                                            device_id={'ep': dev_l if d else dev_r}, device_id_type=MESH)

    def send_f(q):
        return pltpu.make_async_remote_copy(acc.at[q * ep_size + mate], fin.at[q], s_f.at[q], r_f.at[q],
                                            device_id={'ep': mate}, device_id_type=MESH)

    def relay(q):
        for d in range(2):
            send_1(q, d).wait_recv()
            block = (left if d else right) * 2 + d
            acc[q * ep_size + block] = acc[q * ep_size + block] + recv1[d, q]
            send_2(q, d).start()

    def weigh(q, m):
        send_y(q, m).wait_recv()
        for j in range(2):
            b = 2 * chip_of(m) + j
            for n in range(side // b_dev):
                cols = slice(n * b_dev, (n + 1) * b_dev)
                acc[q * ep_size + b, :, cols] = (share[b] * ybuf[lax.rem(q, 2), core, b, :, cols].astype(F32)
                                                 + share[ep_size + b] * yrecv[q, b, :, cols].astype(F32))

    @pl.loop(0, SPLIT)
    def _(q):
        @pl.when(q > 0)
        def _():
            @pl.loop(0, groups)
            def _(g):
                down(q, g)

        @pl.when(q > 1)
        def _():
            for m in range(n_chip):
                send_y(q - 2, m).wait_send()

        @pl.loop(0, n_chip)
        def _(m):
            rows = pl.ds(pl.multiple_of(chip_of(m) * (2 * b_dev), 2 * b_dev), 2 * b_dev)
            back = jnp.dot(perm[rows, :], ys[...], preferred_element_type=F32).astype(BF16)
            for h in range(2):
                ybuf[lax.rem(q, 2), h, pl.ds(2 * chip_of(m), 2)] = back[:, h * side:(h + 1) * side].reshape(2, b_dev, side)
            send_y(q, m).start()

        weigh(q, 0)
        send_1(q, 0).start()
        send_1(q, 1).start()

        @pl.when(q > 0)
        def _():
            relay(q - 1)

        for m in range(1, n_chip):
            weigh(q, m)

    relay(SPLIT - 1)

    def columns(q, which):
        return pl.ds(pl.multiple_of(q * wide + which * side, side), side)

    @pl.loop(0, SPLIT)
    def _(q):
        send_2(q, 0).wait_recv()
        send_2(q, 1).wait_recv()
        acc[q * ep_size + mate] = acc[q * ep_size + mate] + recv2[0, q, 1 - core] + recv2[1, q, 1 - core]
        send_f(q).start()
        mine = acc[q * ep_size + me] + recv2[0, q, core] + recv2[1, q, core]
        cols = columns(q, core)
        out_ref[:, cols] = (x_ref[:, cols].astype(F32) + mine).astype(BF16)

    @pl.loop(0, SPLIT)
    def _(q):
        send_f(q).wait_recv()
        cols = columns(q, 1 - core)
        out_ref[:, cols] = (x_ref[:, cols].astype(F32) + fin[q]).astype(BF16)

    for k in range(1, ep_size):
        send_meta(k).wait_send()
    for k in range(DEEP):
        for i, (h, target) in enumerate(outgoing):
            send_own(k, h, target, i).wait_send()
        for i, (src, h, target) in enumerate(passed + handed):
            forward(k, src, h, target, i).wait_send()

    @pl.loop(0, SPLIT)
    def _(q):
        @pl.when(q >= SPLIT - 2)
        def _():
            for m in range(n_chip):
                send_y(q, m).wait_send()

        send_f(q).wait_send()
        for d in range(2):
            send_1(q, d).wait_send()
            send_2(q, d).wait_send()


def moe_block(ep_size, h_moe, x_mid, meta, w_gate, w_up, w_down):
    b_dev, hidden = h_moe.shape
    e_local, _, ff = w_gate.shape
    wide, side = hidden // SPLIT, hidden // SPLIT // 2
    n_a, n_b, per = 4, 3, 4
    depth, n_ff = hidden // DEEP, ff // side
    vmem, dma = pltpu.VMEM, pltpu.SemaphoreType.DMA
    tokens = ep_size * b_dev
    return pl.pallas_call(
        functools.partial(moe_kernel, ep_size),
        out_shape=(jax.ShapeDtypeStruct((b_dev, hidden), BF16), jax.ShapeDtypeStruct((1,), F32)),
        in_specs=[pl.BlockSpec(memory_space=pltpu.VMEM)] * 3 + [pl.BlockSpec(memory_space=pl.ANY)] * 3,
        out_specs=(pl.BlockSpec(memory_space=pltpu.VMEM), pl.BlockSpec(memory_space=pltpu.SMEM)),
        scratch_shapes=[
            vmem((DEEP, ep_size, b_dev, depth), BF16), vmem((ep_size, 2 * ep_size, b_dev), F32),
            vmem((tokens, e_local * SEATS), BF16), vmem((b_dev, b_dev), F32), vmem((2 * ep_size, b_dev, b_dev), F32),
            vmem((SEATS, depth), BF16), vmem((SEATS, depth), BF16), vmem((e_local, SEATS, ff), BF16), vmem((e_local * SEATS, wide), BF16),
            vmem((2, 2, ep_size, b_dev, side), BF16), vmem((SPLIT, ep_size, b_dev, side), BF16),
            vmem((max(e_local * 2 * n_ff, SPLIT * ep_size), b_dev, side), F32), vmem((2, SPLIT, b_dev, side), F32),
            vmem((2, SPLIT, 2, b_dev, side), F32), vmem((SPLIT, b_dev, side), F32),
            vmem((n_a, depth, ff), BF16), vmem((n_a, depth, ff), BF16), vmem((n_b, per, ff, wide), BF16),
            dma((2, n_a)), dma((n_b,)), dma((DEEP, 6)), dma((DEEP, 8)), dma((DEEP, ep_size, 2)),
            dma((ep_size - 1,)), dma((ep_size,)),
            dma((SPLIT, ep_size // 2)), dma((SPLIT, ep_size // 2)), dma((2, SPLIT)), dma((2, SPLIT)), dma((2, SPLIT)), dma((2, SPLIT)),
            dma((SPLIT,)), dma((SPLIT,)),
        ],
        compiler_params=pltpu.CompilerParams(collective_id=0, has_side_effects=True, vmem_limit_bytes=67043328),
        name='moe',
    )(h_moe, x_mid, meta, w_gate, w_up, w_down)


def moe_general(ep_size, h_moe, x_mid, meta, w_gate, w_up, w_down):
    b_dev, hidden = h_moe.shape
    rows = lax.all_to_all(jnp.broadcast_to(h_moe[None], (ep_size, b_dev, hidden)), 'ep', 0, 0, tiled=True)
    rows = rows.reshape(ep_size * b_dev, hidden)
    ids = lax.all_to_all(meta[:ep_size, None, :], 'ep', 0, 0, tiled=True).reshape(ep_size * b_dev)

    def one(e, done):
        gate = jnp.dot(rows, w_gate[e], preferred_element_type=F32)
        up = jnp.dot(rows, w_up[e], preferred_element_type=F32)
        act = (jax.nn.silu(gate) * up).astype(BF16)
        y = jnp.dot(act, w_down[e], preferred_element_type=F32).astype(BF16)
        return jnp.where((ids == e.astype(F32))[:, None], y, done)

    y = lax.fori_loop(0, w_gate.shape[0], one, jnp.zeros(rows.shape, BF16))
    back = lax.all_to_all(y.reshape(ep_size, b_dev, hidden), 'ep', 0, 0, tiled=True)
    total = jnp.sum(back.astype(F32) * meta[ep_size:, :, None], axis=0)
    return (x_mid.astype(F32) + total).astype(BF16)


def solution(mesh):
    ep_size = mesh.shape['ep']
    row_spec = P(('dp', 'ep'))
    replicated = P()
    expert_spec = P('ep')
    in_specs = (row_spec,) * 5 + (replicated,) * 9 + (expert_spec,) * 3
    out_specs = (row_spec, row_spec, row_spec)

    def device_step(x_in, k_cache, v_cache, cache_len, topk_idx, ln_attn, w_q, w_k, w_v, q_norm, k_norm, w_o, ln_moe, w_router, w_gate, w_up, w_down):
        x_mid, h_moe, meta, k_full, v_full = attend_block(
            ep_size, x_in, k_cache, v_cache, cache_len, topk_idx, ln_attn, w_q, w_k, w_v, q_norm, k_norm, w_o, ln_moe, w_router)
        fast, most = moe_block(ep_size, h_moe, x_mid, meta, w_gate, w_up, w_down)
        x_out = lax.while_loop(
            lambda state: state[0][0] > SEATS,
            lambda state: (jnp.zeros_like(state[0]), moe_general(ep_size, h_moe, x_mid, meta, w_gate, w_up, w_down)),
            (most, fast))[1]
        return x_out, k_full, v_full

    return jax.shard_map(device_step, mesh=mesh, in_specs=in_specs, out_specs=out_specs, check_vma=False)
```

time: 145 us -> 127 us (0.88)
  Pallas kernels: 136 us -> 124 us
  local copies, waits for them, and re-layouts: 5.71 us -> 1.88 us
  other arithmetic: 1.74 us -> 0 us
    pallas_call x1, Pallas kernels: 105 us -> 97.7 us  [moe_block(): pl.pallas_call(functools.partial(moe_kernel, ep_size), out_shape=(jax.Sha...]
    pallas_call x1, Pallas kernels: 31.1 us -> 25.9 us  [attend_block(): pl.pallas_call(functools.partial(attend_kernel, ep_size), out_shape=(jax....]
    broadcast_in_dim x2 -> x0, local copies, waits for them, and re-layouts: 2.58 us -> none  [the longest x1 1.3 us: attend_block(): ln_moe[None]]
where the time goes in v3:
time: 127 us
  Pallas kernels  124 us (98%)
  local copies, waits for them, and re-layouts  1.88 us (1%)
    pallas_call x1, Pallas kernels, moe_block(): pl.pallas_call(functools.partial(moe_kernel, ep_size), out_shape=(jax.Sha...  97.7 us
    pallas_call x1, Pallas kernels, attend_block(): pl.pallas_call(functools.partial(attend_kernel, ep_size), out_shape=(jax....  25.9 us

profile of v3, /device:TPU:113, one launch (start us, length us, event | category | flops | bytes accessed | tf_op | source)
XLA Modules:
  0.0 126.9 jit_solution(15957859262304850573)
XLA Ops:
  0.6 25.9 %attend.1 = (bf16[128,2048]{1,0:T(8,128)(2,1)}, bf16[128,2048]{1,0:T(8,128)(2,1)}, f32[16,128]{1,0:T(8,128)}, bf16[128,128,128]{2,1,0:T(8,128)(2,1)}, bf16[128,128,128]{2,1,0:T(8,128)(2,1)}) custom-call(s32[128]{0:T(128)} %len_ref.1, bf16[128,2048]{1,0:T(8,128)(2,1)} %x_ref.1, s32[1,128]{1,0:T(1,128)} %bitcast.73, s32[8,128]{1,0:T(8,128)} %bitcast.70, ...), custom_call_target="tpu_custom_call" | custom-call | tf_op jit(solution)/shard_map/attend/pallas_call | solution.py:187
  26.6 97.7 %moe.1 = (bf16[128,2048]{1,0:T(8,128)(2,1)}, f32[1]{0:T(128)}) custom-call(bf16[128,2048]{1,0:T(8,128)(2,1)} %get-tuple-element.319.h_ref, bf16[128,2048]{1,0:T(8,128)(2,1)} %get-tuple-element.318.x_ref, f32[16,128]{1,0:T(8,128)} %get-tuple-element.320.meta_ref, bf16[16,2048,768]{2,1,0:T(8,128)(2,1)} %wg_hbm.1, bf16[16,2048,768]{2,1,0:T(8,128)(2,1)} %wu_hbm.1, ...), custom_call_target="tpu_custom_call" | custom-call | tf_op jit(solution)/shard_map/moe/pallas_call | solution.py:547
  124.3 0.7 while.21
  125.0 1.9 %copy.35 = bf16[128,2048]{1,0:T(8,128)(2,1)} copy(bf16[128,2048]{1,0:T(8,128)(2,1)} %get-tuple-element.343) | data formatting | bytes 1048576

commit v4 on v3

--- a/solution.py
+++ b/solution.py
@@ -42,16 +42,17 @@
     n_q, n_o = s_q.shape[0], s_o.shape[0]
     n_blk = s_c.shape[1]
     blk = b_dev // n_blk
-    qc, oc = q_width // n_q, hidden // n_o
+    deep, qc, oc = hidden // n_q, part.shape[2], hidden // 2
+    n_part = q_width // qc
     rep = q_heads // kv_heads
 
     def copy_q(i):
-        cols = pl.ds(pl.multiple_of(i * qc, qc), qc)
-        return pltpu.make_async_copy(wq_hbm.at[:, cols], wq.at[:, cols], s_q.at[i])
+        rows = pl.ds(i * deep, deep)
+        return pltpu.make_async_copy(wq_hbm.at[rows], wq.at[rows], s_q.at[i])
 
     def copy_o(i):
-        cols = pl.ds(pl.multiple_of(i * oc, oc), oc)
-        return pltpu.make_async_copy(wo_hbm.at[:, cols], wo.at[:, cols], s_o.at[i])
+        rows = pl.ds(i * (q_width // n_o), q_width // n_o)
+        return pltpu.make_async_copy(wo_hbm.at[rows], wo.at[rows], s_o.at[i])
 
     def copy_in(b):
         rows = pl.ds(b * blk, blk)
@@ -69,6 +70,9 @@
         c.start()
     for i in range(n_q):
         copy_q(i).start()
+    for b in range(n_blk):
+        for c in copy_in(b):
+            c.start()
 
     x = x_ref[...].astype(F32)
     rms_rows(x, lna_ref, hn)
@@ -100,18 +104,14 @@
 
     for i in range(n_q):
         copy_q(i).wait()
-        if i == 1:
-            for b in range(n_blk):
-                for c in copy_in(b):
-                    c.start()
-        if i == 4:
-            for j in range(n_o):
-                copy_o(j).start()
-            small[2].start()
+    for i in range(n_o):
+        copy_o(i).start()
+    small[2].start()
+    for i in range(n_part):
         part[i % 2] = jnp.dot(hn[...], wq[:, i * qc:(i + 1) * qc], preferred_element_type=F32)
         if i:
             spread(i - 1)
-    spread(n_q - 1)
+    spread(n_part - 1)
 
     row_slot = lax.broadcasted_iota(jnp.int32, (lanes, dim), 0) // kv_heads
     lane = lax.broadcasted_iota(jnp.int32, (q_heads, lanes), 1)
@@ -150,6 +150,7 @@
         att[:, h * dim:(h + 1) * dim] = os[pl.ds(h, b_dev, stride=q_heads), :].astype(BF16)
     for i in range(n_o):
         copy_o(i).wait()
+    for i in range(hidden // oc):
         cols = slice(i * oc, (i + 1) * oc)
         out = jnp.dot(att[...], wo[:, cols], preferred_element_type=F32)
         xmid_ref[:, cols] = (x_ref[:, cols].astype(F32) + out).astype(BF16)
@@ -180,7 +181,7 @@
     q_width, kv_width, experts = w_q.shape[1], w_k.shape[1], w_router.shape[1]
     q_heads = q_width // dim
     lanes = n_slots * kv_heads
-    n_q, n_o, n_blk = 8, 4, 8
+    n_q, n_o, n_blk = 8, 4, 2
     vmem, dma, far = pltpu.VMEM, pltpu.SemaphoreType.DMA, pl.BlockSpec(memory_space=pl.ANY)
     near = pl.BlockSpec(memory_space=pltpu.VMEM)
     flat = (b_dev, lanes, dim)
@@ -196,7 +197,7 @@
             vmem((q_width, hidden), BF16), vmem((hidden, experts), BF16), vmem(flat, BF16), vmem(flat, BF16),
             vmem((b_dev * q_heads, dim), F32), vmem((b_dev * q_heads, dim), F32),
             vmem((b_dev * 8, dim), F32), vmem((b_dev * 8, dim), F32),
-            vmem((b_dev, hidden), BF16), vmem((b_dev, q_width), BF16), vmem((2, b_dev, q_width // n_q), F32),
+            vmem((b_dev, hidden), BF16), vmem((b_dev, q_width), BF16), vmem((2, b_dev, q_width // 8), F32),
             dma((n_q,)), dma((3,)), dma((n_o,)), dma((2, n_blk)), dma((2, n_blk)),
         ],
         compiler_params=pltpu.CompilerParams(vmem_limit_bytes=67043328),
@@ -335,7 +336,7 @@
 
     seat_cols = lax.broadcasted_iota(jnp.int32, (b_dev, 4 * SEATS), 1).astype(F32)
     for b in range(ep_size):
-        col = jnp.transpose(keys[...])[:, b:b + 1]
+        col = keyt[:, b:b + 1]
 
         @pl.loop(0, e_local // 4)
         def _(j):
@@ -407,13 +408,13 @@
                 project(k, e, now)
                 refill(k * e_local + e)
             if k + 1 < DEEP:
-                @pl.when(p == 0)
+                @pl.when(p == 1)
                 def _():
                     pump(k + 1)
                     if k + 2 < DEEP:
                         own(k + 2)
 
-                @pl.when(p == 3)
+                @pl.when(p == 4)
                 def _():
                     hand(k + 1)
             else:
@@ -540,7 +541,7 @@
     b_dev, hidden = h_moe.shape
     e_local, _, ff = w_gate.shape
     wide, side = hidden // SPLIT, hidden // SPLIT // 2
-    n_a, n_b, per = 4, 3, 4
+    n_a, n_b, per = 5, 3, 4
     depth, n_ff = hidden // DEEP, ff // side
     vmem, dma = pltpu.VMEM, pltpu.SemaphoreType.DMA
     tokens = ep_size * b_dev

time: 127 us -> 124 us (0.976)
  Pallas kernels: 124 us -> 120 us
    pallas_call x1, Pallas kernels: 25.9 us -> 23.6 us  [attend_block(): pl.pallas_call(functools.partial(attend_kernel, ep_size), out_shape=(jax....]
where the time goes in v4:
time: 124 us
  Pallas kernels  120 us (97%)
  local copies, waits for them, and re-layouts  1.88 us (2%)
    pallas_call x1, Pallas kernels, moe_block(): pl.pallas_call(functools.partial(moe_kernel, ep_size), out_shape=(jax.Sha...  96.7 us
    pallas_call x1, Pallas kernels, attend_block(): pl.pallas_call(functools.partial(attend_kernel, ep_size), out_shape=(jax....  23.6 us

profile of v4, /device:TPU:113, one launch (start us, length us, event | category | flops | bytes accessed | tf_op | source)
XLA Modules:
  0.0 123.6 jit_solution(10925389759252899510)
XLA Ops:
  0.6 23.6 %attend.1 = (bf16[128,2048]{1,0:T(8,128)(2,1)}, bf16[128,2048]{1,0:T(8,128)(2,1)}, f32[16,128]{1,0:T(8,128)}, bf16[128,128,128]{2,1,0:T(8,128)(2,1)}, bf16[128,128,128]{2,1,0:T(8,128)(2,1)}) custom-call(s32[128]{0:T(128)} %len_ref.1, bf16[128,2048]{1,0:T(8,128)(2,1)} %x_ref.1, s32[1,128]{1,0:T(1,128)} %bitcast.73, s32[8,128]{1,0:T(8,128)} %bitcast.70, ...), custom_call_target="tpu_custom_call" | custom-call | tf_op jit(solution)/shard_map/attend/pallas_call | solution.py:188
  24.3 96.7 %moe.1 = (bf16[128,2048]{1,0:T(8,128)(2,1)}, f32[1]{0:T(128)}) custom-call(bf16[128,2048]{1,0:T(8,128)(2,1)} %get-tuple-element.319.h_ref, bf16[128,2048]{1,0:T(8,128)(2,1)} %get-tuple-element.318.x_ref, f32[16,128]{1,0:T(8,128)} %get-tuple-element.320.meta_ref, bf16[16,2048,768]{2,1,0:T(8,128)(2,1)} %wg_hbm.1, bf16[16,2048,768]{2,1,0:T(8,128)(2,1)} %wu_hbm.1, ...), custom_call_target="tpu_custom_call" | custom-call | tf_op jit(solution)/shard_map/moe/pallas_call | solution.py:548
  121.0 0.7 while.21
  121.7 1.9 %copy.35 = bf16[128,2048]{1,0:T(8,128)(2,1)} copy(bf16[128,2048]{1,0:T(8,128)(2,1)} %get-tuple-element.343) | data formatting | bytes 1048576
